TPU v7x, 256 devices: a 2x2x32 block of a 4x8x32 slice. The times are simulated.
256 devices in a mesh: replica: 4 (over y, x), seq: 64 (over z, core).
Axes of the slice: x: 2, y: 2, z: 32, core: 2. Of those that a mesh axis runs over, the one named last changes fastest.
The devices are a block of a 4x8x32 slice.
Arguments:
- hidden_in: bfloat16 [64, 8192], P('replica'), parts along dimension 0, may hold values from -6 to 6
- w_query: bfloat16 [8192, 8192], P(None, 'seq'), may hold values from -1 to 1
- w_keyval: bfloat16 [8192, 2048], P(None, 'seq'), may hold values from -0.1875 to 0.1875
- key_cache: bfloat16 [64, 8192, 1024], P('replica', 'seq'), parts along dimension 0, may hold values from -15 to 15
- value_cache: bfloat16 [64, 8192, 1024], P('replica', 'seq'), parts along dimension 0, may hold values from -6 to 6
- lengths: int32 [64], P('replica'), parts along dimension 0, may hold values from 128 to 8191, as said below
- w_out: bfloat16 [8192, 8192], P('seq'), may hold values from -0.1875 to 0.1875
Outputs:
- attn_out: bfloat16 [64, 8192], P('replica', 'seq'), parts along dimension 0
There are 4 independent parts, one for each index of `replica`. A program takes and returns all parts, laid end to end along the dimension named above; an argument that names none is the same for every part. Nothing has to cross between parts.
Inputs may be any that keep to these rules, and one draw needn't show every extreme that they name: The new token of sequence b is written at position lengths[b]; it attends to positions 0 to lengths[b].
All inputs are finite; a program needn't handle non-finite values.
Results may differ from a plain program's by a relative error of at most 0.013.
Values may be sent and summed in bfloat16 or wider, within the bound.
No kernel may reach another device: no remote copies, remote signals or barrier semaphores. Data moves between devices by JAX's collectives and lax.ppermute only.
A program may use at most 64 MiB of HBM per device.

v0:
```python
import math

import jax
import jax.numpy as jnp
from jax import lax
from jax.sharding import PartitionSpec as P

KV_HEADS = 8
HEAD_DIM = 128


def joined_along(pieces, dim):
    pieces = jnp.moveaxis(pieces, 0, dim)
    shape = pieces.shape
    return pieces.reshape(*shape[:dim], shape[dim] * shape[dim + 1], *shape[dim + 2 :])


def gather_together(arrays, axis, dims):
    ravelled = jnp.concatenate([a.reshape(-1) for a in arrays])
    lines, at, finished = (lax.all_gather(ravelled, axis), 0, [])
    for a, dim in zip(arrays, dims):
        pieces = lines[:, at : at + a.size].reshape(-1, *a.shape)
        finished.append(joined_along(pieces, dim))
        at += a.size
    return tuple(finished)


def split_up(x, dim, peers):
    before, after = (x.shape[:dim], x.shape[dim + 1 :])
    return jnp.moveaxis(x.reshape(*before, peers, -1, *after), dim, 0)


def sum_at_owner(x, axis, dim):
    pieces = split_up(x, dim, lax.axis_size(axis))
    arrived = lax.all_to_all(pieces, axis, split_axis=0, concat_axis=0, tiled=True)
    return arrived.sum(axis=0)


def regroup_merge(pieces):
    out_parts, max_parts, sum_parts = pieces
    largest = jnp.max(max_parts, axis=0)
    factor = jnp.exp(max_parts - largest[None])
    numerator = jnp.sum(out_parts * factor[..., None], axis=0)
    denominator = jnp.sum(sum_parts * factor, axis=0)
    return numerator / denominator[..., None]


def body(hidden_in, w_query, w_keyval, key_cache, value_cache, lengths, w_out):
    batch_rows, ctx_dev, half_width = key_cache.shape
    shards = lax.axis_size("seq")
    shard_index = lax.axis_index("seq")
    heads_dev = w_out.shape[0] // HEAD_DIM
    all_heads = heads_dev * shards
    group_size = all_heads // KV_HEADS
    query_part = jnp.dot(hidden_in, w_query, preferred_element_type=jnp.float32).astype(
        jnp.bfloat16
    )
    keyval_part = jnp.dot(hidden_in, w_keyval, preferred_element_type=jnp.float32).astype(
        jnp.bfloat16
    )
    query, new_kv = gather_together((query_part, keyval_part), "seq", (1, 1))
    first_slot = shard_index * ctx_dev
    slot_ids = first_slot + lax.broadcasted_iota(jnp.int32, (batch_rows, ctx_dev), 1)
    is_new = (slot_ids == lengths[:, None])[..., None]
    key_rows = jnp.where(is_new, new_kv[:, None, :half_width], key_cache)
    value_rows = jnp.where(is_new, new_kv[:, None, half_width:], value_cache)
    grouped = query.reshape(batch_rows, KV_HEADS, group_size, HEAD_DIM)
    key_heads = key_rows.reshape(batch_rows, ctx_dev, KV_HEADS, HEAD_DIM)
    value_heads = value_rows.reshape(batch_rows, ctx_dev, KV_HEADS, HEAD_DIM)
    scores = jnp.einsum("bkgd,btkd->bkgt", grouped, key_heads, preferred_element_type=jnp.float32)
    scores = scores / math.sqrt(HEAD_DIM)
    used = (slot_ids <= lengths[:, None])[:, None, None, :]
    scores = jnp.where(used, scores, -1e30)
    local_max = jnp.max(scores, axis=-1)
    weights = jnp.exp(scores - local_max[..., None])
    local_sum = jnp.sum(weights, axis=-1)
    local_out = jnp.einsum(
        "bkgt,btkd->bkgd",
        weights.astype(jnp.bfloat16),
        value_heads,
        preferred_element_type=jnp.float32,
    )
    local_max = local_max.reshape(batch_rows, all_heads)
    local_sum = local_sum.reshape(batch_rows, all_heads)
    local_out = local_out.reshape(batch_rows, all_heads, HEAD_DIM)
    merged = regroup_merge(
        (
            lax.all_to_all(local_out[None], "seq", split_axis=2, concat_axis=0, tiled=True),
            lax.all_to_all(local_max[None], "seq", split_axis=2, concat_axis=0, tiled=True),
            lax.all_to_all(local_sum[None], "seq", split_axis=2, concat_axis=0, tiled=True),
        )
    )
    attended = merged.reshape(batch_rows, heads_dev * HEAD_DIM).astype(jnp.bfloat16)
    term = jnp.dot(attended, w_out, preferred_element_type=jnp.float32)
    return sum_at_owner(term, "seq", 1).astype(jnp.bfloat16)


def solution(mesh):
    placed = (
        P("replica", None),
        P(None, "seq"),
        P(None, "seq"),
        P("replica", "seq", None),
        P("replica", "seq", None),
        P("replica"),
        P("seq", None),
    )
    return jax.shard_map(
        body, mesh=mesh, in_specs=placed, out_specs=P("replica", "seq"), check_vma=False
    )
```

profile of v0, /device:TPU:38, one launch (start us, length us, event | category | flops | bytes accessed | tf_op | source)
XLA Modules:
  0.0 295.8 jit_solution(3737020876434760539)
XLA Ops:
  0.0 0.0 copy-start
  0.0 0.0 copy-start.1
  0.0 1.5 convolution_convert_fusion
  1.5 0.1 reshape.198
  1.6 0.2 copy-done
  1.8 1.3 fusion.15
  3.2 76.9 %all-gather.1 = bf16[64,1,2560]{2,1,0:T(2,128)(2,1)S(1)} all-gather(bf16[1,1,2560]{2,1,0:T(2,128)(2,1)S(1)} %reshape.205), channel_id=2, replica_groups=mesh['replica'=4,'seq'=64] {'seq'}, dimensions={0}, use_global_device_ids=true | all-gather | bytes 332800 | tf_op jit(solution)/shard_map/all_gather | solution.py:20
  80.2 0.1 copy.20
  80.3 0.2 copy.21
  80.5 0.3 reshape.201
  80.9 0.0 copy-done.1
  80.9 0.1 broadcast_compare_fusion.1
  80.9 5.1 %select_bitcast_fusion.1 = (bf16[16,16,8,8,128]{4,3,2,1,0:T(8,128)(2,1)S(1)}, bf16[16,16,8,8,128]{4,3,2,1,0:T(8,128)(2,1)}) fusion(bf16[16,128,1024]{2,1,0:T(8,128)(2,1)} %param.10, pred[16,128]{1,0:T(8,128)(4,1)S(1)} %get-tuple-element.10, bf16[16,1024]{1,0:T(8,128)(2,1)S(1)} %get-tuple-element.5, bf16[16,128,1024]{2,1,0:T(8,128)(2,1)} %param.11, ...), kind=kLoop, calls=%fused_computation.7 | loop fusion | flops 4194304 | bytes 16844800
  86.1 2.3 fusion.30
  88.4 0.7 copy.25
  89.1 12.4 %all-to-all-start.1 = ((f32[1,16,64]{1,0,2:T(1,128)}), f32[1,16,64]{1,0,2:T(1,128)S(1)}, u32[]{:S(2)}, u32[]{:S(2)}) async-start(f32[1,16,64]{1,0,2:T(1,128)} %bitcast.10), calls=%async_computation.1 | async-start | bytes 65536 | tf_op jit(solution)/shard_map/all_to_all | solution.py:89
  101.6 0.4 fusion.17
  102.0 0.7 copy.27
  102.7 20.9 %all-to-all-done.1 = f32[1,16,64]{1,0,2:T(1,128)S(1)} async-done(((f32[1,16,64]{1,0,2:T(1,128)}), f32[1,16,64]{1,0,2:T(1,128)S(1)}, u32[]{:S(2)}, u32[]{:S(2)}) %all-to-all-start.1) | async-done | bytes 4128 | tf_op jit(solution)/shard_map/all_to_all | solution.py:89
  123.6 6.4 %all-to-all-start.2 = ((f32[1,16,64]{1,0,2:T(1,128)}), f32[1,16,64]{1,0,2:T(1,128)S(1)}, u32[]{:S(2)}, u32[]{:S(2)}) async-start(f32[1,16,64]{1,0,2:T(1,128)} %bitcast.16), calls=%async_computation.2 | async-start | bytes 65536 | tf_op jit(solution)/shard_map/all_to_all | solution.py:90
  130.0 3.4 %fusion.6 = f32[1,16,64,128]{3,2,1,0:T(8,128)S(1)} fusion(bf16[16,16,8,8,128]{4,3,2,1,0:T(8,128)(2,1)} %get-tuple-element.8, f32[16,8,8,128]{3,2,1,0:T(8,128)S(1)} %get-tuple-element.12, f32[16,8,8]{2,1,0:T(8,128)S(1)} %get-tuple-element.11), kind=kOutput, calls=%fused_computation.9 | convolution fusion | flops 33816576 | bytes 5246976 | tf_op jit(solution)/shard_map/bkgt,btkd->bkgd/dot_general | solution.py:77
  133.4 1.1 copy.24
  134.5 17.4 %all-to-all-done.2 = f32[1,16,64]{1,0,2:T(1,128)S(1)} async-done(((f32[1,16,64]{1,0,2:T(1,128)}), f32[1,16,64]{1,0,2:T(1,128)S(1)}, u32[]{:S(2)}, u32[]{:S(2)}) %all-to-all-start.2) | async-done | bytes 4128 | tf_op jit(solution)/shard_map/all_to_all | solution.py:90
  152.0 6.7 %all-to-all-start = ((f32[1,16,64,128]{3,1,0,2:T(8,128)}), f32[1,16,64,128]{3,1,0,2:T(8,128)S(1)}, u32[]{:S(2)}, u32[]{:S(2)}) async-start(f32[1,16,64,128]{3,1,0,2:T(8,128)} %copy.24), calls=%async_computation | async-start | bytes 1048576 | tf_op jit(solution)/shard_map/all_to_all | solution.py:88
  158.6 4.1 %copy.30 = bf16[8192,128]{1,0:T(8,128)(2,1)} copy(bf16[8192,128]{0,1:T(8,128)(2,1)} %bitcast.96) | data formatting | bytes 4194304 | tf_op jit(solution)/shard_map/dot_general | solution.py:94
  162.8 0.1 reduce_max.19
  162.9 59.8 %all-to-all-done = f32[1,16,64,128]{3,1,0,2:T(8,128)S(1)} async-done(((f32[1,16,64,128]{3,1,0,2:T(8,128)}), f32[1,16,64,128]{3,1,0,2:T(8,128)S(1)}, u32[]{:S(2)}, u32[]{:S(2)}) %all-to-all-start) | async-done | bytes 524320 | tf_op jit(solution)/shard_map/all_to_all | solution.py:88
  222.7 0.2 fusion.16
  222.9 2.3 convolution_bitcast_fusion
  225.2 69.9 %all_to_all.62 = f32[64,16,128]{2,1,0:T(8,128)S(1)} all-to-all(f32[64,16,128]{2,1,0:T(8,128)S(1)} %convolution_bitcast_fusion), channel_id=1, replica_groups=mesh['replica'=4,'seq'=64] {'seq'}, dimensions={0} | all-to-all | bytes 1048576 | tf_op jit(solution)/shard_map/all_to_all | solution.py:35
  295.1 0.7 reduce_sum.42
  (10 shorter events, 0.2 us)
Async XLA Ops:
  0.0 1.8 copy-start
  0.0 80.9 %copy-start.1 = (s32[16]{0:T(128)S(1)}, s32[16]{0:T(128)}, u32[]{:S(2)}) copy-start(s32[16]{0:T(128)} %param.12) | copy-start | bytes 196
  89.1 34.4 %all-to-all-start.1 = ((f32[1,16,64]{1,0,2:T(1,128)}), f32[1,16,64]{1,0,2:T(1,128)S(1)}, u32[]{:S(2)}, u32[]{:S(2)}) async-start(f32[1,16,64]{1,0,2:T(1,128)} %bitcast.10), calls=%async_computation.1 | async-start | bytes 65536 | tf_op jit(solution)/shard_map/all_to_all | solution.py:89
  123.6 28.4 %all-to-all-start.2 = ((f32[1,16,64]{1,0,2:T(1,128)}), f32[1,16,64]{1,0,2:T(1,128)S(1)}, u32[]{:S(2)}, u32[]{:S(2)}) async-start(f32[1,16,64]{1,0,2:T(1,128)} %bitcast.16), calls=%async_computation.2 | async-start | bytes 65536 | tf_op jit(solution)/shard_map/all_to_all | solution.py:90
  152.0 70.7 %all-to-all-start = ((f32[1,16,64,128]{3,1,0,2:T(8,128)}), f32[1,16,64,128]{3,1,0,2:T(8,128)S(1)}, u32[]{:S(2)}, u32[]{:S(2)}) async-start(f32[1,16,64,128]{3,1,0,2:T(8,128)} %copy.24), calls=%async_computation | async-start | bytes 1048576 | tf_op jit(solution)/shard_map/all_to_all | solution.py:88
where the time goes:
time: 296 us
  blocking collectives  147 us (50%)
  waiting for transfers between devices  98.1 us (33%)
  starting transfers between devices  25.5 us (9%)
  matrix products  10.9 us (4%)
  local copies, waits for them, and re-layouts  7.65 us (3%)
  other arithmetic  6.61 us (2%)
    all_gather x1, blocking collectives, gather_together(): lines, at, finished = (lax.all_gather(ravelled, axis), 0, [])  76.9 us
    all_to_all x1, blocking collectives, sum_at_owner(): lax.all_to_all(pieces, axis, split_axis=0, concat_axis=0, tiled=True)  69.9 us
    all_to_all x1, waiting for transfers between devices, body(): lax.all_to_all(local_out[None], 'seq', split_axis=2, concat_axis=0, tiled...  59.8 us
    all_to_all x1, waiting for transfers between devices, body(): lax.all_to_all(local_max[None], 'seq', split_axis=2, concat_axis=0, tiled...  20.9 us
    all_to_all x1, waiting for transfers between devices, body(): lax.all_to_all(local_sum[None], 'seq', split_axis=2, concat_axis=0, tiled...  17.4 us
    all_to_all x1, starting transfers between devices, body(): lax.all_to_all(local_max[None], 'seq', split_axis=2, concat_axis=0, tiled...  12.4 us
    all_to_all x1, starting transfers between devices, body(): lax.all_to_all(local_out[None], 'seq', split_axis=2, concat_axis=0, tiled...  6.67 us
    all_to_all x1, starting transfers between devices, body(): lax.all_to_all(local_sum[None], 'seq', split_axis=2, concat_axis=0, tiled...  6.4 us
  transfers between devices with their start and end apart: 3, of which 3 were waited for; matrix products, arithmetic and copies ran while one was open for 3% of the time, Pallas kernels for 0%

commit v1 on v0

v1 whole, which is shorter than its diff:
```python
import math

import jax
import jax.numpy as jnp
from jax import lax
from jax.sharding import PartitionSpec as P

KV_HEADS = 8
HEAD_DIM = 128
CORES = 2
NEAR = 4
EMPTY = -1e30


def same_core_groups(shards):
    return [[CORES * z + c for z in range(shards // CORES)] for c in range(CORES)]


def near_groups(shards):
    blocks = shards // CORES // NEAR
    return [
        [CORES * (NEAR * b + i) + c for i in range(NEAR)] for b in range(blocks) for c in range(CORES)
    ]


def far_groups(shards):
    blocks = shards // CORES // NEAR
    return [
        [CORES * (NEAR * b + i) + c for b in range(blocks)] for i in range(NEAR) for c in range(CORES)
    ]


def exchange(x, groups):
    return lax.all_to_all(
        x, "seq", split_axis=0, concat_axis=0, axis_index_groups=groups, tiled=True
    )


def to_partner(x, shards):
    return lax.ppermute(x, "seq", [(i, i ^ 1) for i in range(shards)])


def rounded(x):
    return lax.reduce_precision(x, exponent_bits=8, mantissa_bits=7)


def split_terms(x):
    high = rounded(x)
    middle = rounded(x - high)
    low = rounded(x - high - middle)
    return high.astype(jnp.bfloat16), middle.astype(jnp.bfloat16), low.astype(jnp.bfloat16)


def body(hidden_in, w_query, w_keyval, key_cache, value_cache, lengths, w_out):
    batch, ctx_dev, half_width = key_cache.shape
    shards = lax.axis_size("seq")
    index = lax.axis_index("seq")
    chips = shards // CORES
    heads = w_out.shape[0] // HEAD_DIM * shards
    group = heads // KV_HEADS
    group_chips = group // CORES
    f32, bf16 = jnp.float32, jnp.bfloat16

    query_part = jnp.dot(hidden_in, w_query, preferred_element_type=f32).astype(bf16)
    keyval_part = jnp.dot(hidden_in, w_keyval, preferred_element_type=f32).astype(bf16)
    kv_cols = keyval_part.shape[1]

    row = jnp.concatenate([query_part.reshape(1, 1, -1), keyval_part.reshape(1, 1, -1)], axis=2)
    width = row.shape[2]
    blocks = chips // NEAR
    far = exchange(jnp.broadcast_to(row, (blocks, 1, width)), far_groups(shards))
    near = exchange(
        jnp.broadcast_to(far[None], (NEAR, blocks, 1, width)).reshape(chips, 1, width),
        near_groups(shards),
    )
    partner = to_partner(near, shards)
    lines = jnp.stack([near, partner]).reshape(CORES, NEAR, blocks, width)
    lines = lines.transpose(2, 1, 0, 3)
    q_size = batch * HEAD_DIM
    query = lines[..., :q_size].reshape(KV_HEADS, group_chips, CORES, batch, HEAD_DIM)
    query = query.transpose(3, 0, 2, 1, 4).reshape(batch, KV_HEADS, group, HEAD_DIM)

    core = index % CORES
    kv_lines = lines[..., q_size:].reshape(chips, CORES, batch, kv_cols)
    kv_lines = jnp.where(core == 0, kv_lines, kv_lines[:, ::-1])
    kv_lines = kv_lines.reshape(2, KV_HEADS, -1, batch, kv_cols)
    own_group = index // group
    own_kv = lax.dynamic_slice_in_dim(kv_lines, own_group, 1, axis=1)[:, 0]
    own_kv = own_kv.transpose(0, 2, 1, 3).reshape(2, batch, HEAD_DIM).astype(f32)
    score_new = jnp.sum(query_part.astype(f32) * own_kv[0], axis=-1) / math.sqrt(HEAD_DIM)

    slots = index * ctx_dev + lax.broadcasted_iota(jnp.int32, (batch, ctx_dev), 1)
    used = (slots < lengths[:, None])[:, None, None, :]
    keys = key_cache.reshape(batch, ctx_dev, KV_HEADS, HEAD_DIM)
    values = value_cache.reshape(batch, ctx_dev, KV_HEADS, HEAD_DIM)
    scores = jnp.einsum("bkgd,btkd->bkgt", query, keys, preferred_element_type=f32)
    scores = jnp.where(used, scores / math.sqrt(HEAD_DIM), EMPTY)
    local_max = jnp.max(scores, axis=-1)
    weights = jnp.where(used, jnp.exp(scores - local_max[..., None]), 0.0)
    local_sum = jnp.sum(weights, axis=-1)
    local_out = jnp.einsum(
        "bkgt,btkd->bkgd", weights.astype(bf16), values, preferred_element_type=f32
    )
    some = local_sum > 0
    scale = jnp.where(some, 1.0 / jnp.where(some, local_sum, 1.0), 0.0)
    level = jnp.where(some, local_max + jnp.log(jnp.where(some, local_sum, 1.0)), EMPTY)
    local_out = local_out * scale[..., None]

    local_out = local_out.reshape(batch, KV_HEADS, CORES, group_chips, HEAD_DIM)
    level = level.reshape(batch, KV_HEADS, CORES, group_chips)
    local_out = local_out.transpose(2, 1, 3, 0, 4).reshape(CORES, chips, batch, HEAD_DIM)
    level = level.transpose(2, 1, 3, 0).reshape(CORES, chips, batch)
    got_out = to_partner(local_out[1].astype(bf16), shards).astype(f32)
    got_level = to_partner(level[1], shards)
    top = jnp.maximum(level[0], got_level)
    part_a = jnp.exp(level[0] - top)
    part_b = jnp.exp(got_level - top)
    whole = part_a + part_b
    merged = (local_out[0] * part_a[..., None] + got_out * part_b[..., None]) / whole[..., None]
    level = jnp.maximum(top + jnp.log(whole), EMPTY)
    stats = jnp.concatenate(split_terms(level), axis=1)
    stats = jnp.pad(stats, ((0, 0), (0, HEAD_DIM - stats.shape[1])))
    packet = jnp.concatenate([merged.astype(bf16).reshape(chips, -1), stats], axis=1)
    arrived = exchange(packet[:, None, :], same_core_groups(shards))[:, 0]
    outs = arrived[:, :q_size].reshape(chips, batch, HEAD_DIM).astype(f32)
    levels = arrived[:, q_size : q_size + 3 * batch].astype(f32).reshape(chips, 3, batch)
    levels = levels[:, 0] + (levels[:, 1] + levels[:, 2])
    top = jnp.maximum(jnp.max(levels, axis=0), score_new)
    factor = jnp.exp(levels - top)
    factor_new = jnp.exp(score_new - top)
    numerator = jnp.sum(outs * factor[..., None], axis=0) + factor_new[:, None] * own_kv[1]
    denominator = jnp.sum(factor, axis=0) + factor_new
    attended = (numerator / denominator[:, None]).astype(bf16)

    term = jnp.dot(attended, w_out, preferred_element_type=f32)
    term = term.reshape(batch, chips, CORES, -1)
    first, second = term[:, :, 0].swapaxes(0, 1), term[:, :, 1].swapaxes(0, 1)
    mine = jnp.where(core == 0, first, second)
    theirs = jnp.where(core == 0, second, first)
    mine = mine + to_partner(theirs.astype(bf16), shards).astype(f32)
    arrived = exchange(mine.astype(bf16), same_core_groups(shards))
    return jnp.sum(arrived.astype(f32), axis=0).astype(bf16)


def solution(mesh):
    placed = (
        P("replica", None),
        P(None, "seq"),
        P(None, "seq"),
        P("replica", "seq", None),
        P("replica", "seq", None),
        P("replica"),
        P("seq", None),
    )
    return jax.shard_map(
        body, mesh=mesh, in_specs=placed, out_specs=P("replica", "seq"), check_vma=False
    )
```

time: 296 us -> 166 us (0.56)
  waiting for transfers between devices: 98.1 us -> 37.6 us
  blocking collectives: 147 us -> 90 us
  starting transfers between devices: 25.5 us -> 9.72 us
    all_gather x1 -> x0, blocking collectives: 76.9 us -> none  [gather_together(): lines, at, finished = (lax.all_gather(ravelled, axis), 0, [])]
    all_to_all x3 -> x2, waiting for transfers between devices: 98.1 us -> 34.2 us  [exchange(): lax.all_to_all(x, 'seq', split_axis=0, concat_axis=0, axis_index_groups=g...]
    all_to_all x1 -> x2, blocking collectives: 69.9 us -> 90 us  [exchange(): lax.all_to_all(x, 'seq', split_axis=0, concat_axis=0, axis_index_groups=g...]
    all_to_all x3 -> x2, starting transfers between devices: 25.5 us -> 8.68 us  [exchange(): lax.all_to_all(x, 'seq', split_axis=0, concat_axis=0, axis_index_groups=g...]
    unnamed x1 -> x0, other arithmetic: 5.13 us -> none
    ppermute x0 -> x4, waiting for transfers between devices: none -> 3.43 us  [to_partner(): return lax.ppermute(x, 'seq', [(i, i ^ 1) for i in range(shards)])]
    unnamed x8 -> x14, local copies, waits for them, and re-layouts: 0.33 us -> 3.6 us
  transfers between devices with their start and end apart: 3 -> 6, of which waited for: 3 -> 5; matrix products, arithmetic and copies ran while one was open for 3% -> 5% of each run, Pallas kernels for 0% -> 0%
where the time goes in v1:
time: 166 us
  blocking collectives  90 us (54%)
  waiting for transfers between devices  37.6 us (23%)
  matrix products  13 us (8%)
  local copies, waits for them, and re-layouts  10.3 us (6%)
  starting transfers between devices  9.72 us (6%)
  other arithmetic  4.85 us (3%)
    all_to_all x2, blocking collectives, exchange(): lax.all_to_all(x, 'seq', split_axis=0, concat_axis=0, axis_index_groups=g...  90 us
    all_to_all x2, waiting for transfers between devices, exchange(): lax.all_to_all(x, 'seq', split_axis=0, concat_axis=0, axis_index_groups=g...  34.2 us
    all_to_all x2, starting transfers between devices, exchange(): lax.all_to_all(x, 'seq', split_axis=0, concat_axis=0, axis_index_groups=g...  8.68 us
    dot_general x1, matrix products, body(): jnp.einsum('bkgd,btkd->bkgt', query, keys, preferred_element_type=f32)  4.53 us
    dot_general x1, local copies, waits for them, and re-layouts, body(): term = jnp.dot(attended, w_out, preferred_element_type=f32)  4.11 us
    unnamed x14, local copies, waits for them, and re-layouts  3.6 us
    dot_general x1, matrix products, body(): jnp.einsum('bkgt,btkd->bkgd', weights.astype(bf16), values, preferred_ele...  3.43 us
    ppermute x4, waiting for transfers between devices, to_partner(): return lax.ppermute(x, 'seq', [(i, i ^ 1) for i in range(shards)])  3.43 us
  transfers between devices with their start and end apart: 6, of which 5 were waited for; matrix products, arithmetic and copies ran while one was open for 5% of the time, Pallas kernels for 0%

profile of v1, /device:TPU:38, one launch (start us, length us, event | category | flops | bytes accessed | tf_op | source)
XLA Modules:
  0.0 165.8 jit_solution(471768609910217131)
XLA Ops:
  0.0 1.6 copy-done
  1.6 1.3 convolution_convert_fusion.1
  2.9 1.4 convolution_convert_fusion
  4.5 0.5 broadcast.101
  5.0 0.9 reduce.5
  5.9 54.7 %all_to_all.20 = bf16[8,2,1280]{2,1,0:T(2,128)(2,1)S(1)} all-to-all(bf16[8,2,1280]{2,1,0:T(2,128)(2,1)S(1)} %reshape.204), channel_id=1, replica_groups={{0,8,16,24,32,40,48,56},{1,9,17,25,33,41,49,57},{2,10,18,26,34,42,50,58..., dimensions={0} | all-to-all | bytes 81920 | tf_op jit(solution)/shard_map/all_to_all | solution.py:34
  60.7 0.7 reduce.6
  61.4 0.7 reshape.206
  62.1 3.9 %all-to-all-start.1 = ((bf16[4,2,10240]{2,1,0:T(2,128)(2,1)}), bf16[4,2,10240]{2,1,0:T(2,128)(2,1)S(1)}, u32[]{:S(2)}, u32[]{:S(2)}) async-start(bf16[4,2,10240]{2,1,0:T(2,128)(2,1)} %reshape.206), calls=%async_computation.1 | async-start | bytes 327680 | tf_op jit(solution)/shard_map/all_to_all | solution.py:34
  66.0 6.0 %all-to-all-done.1 = bf16[4,2,10240]{2,1,0:T(2,128)(2,1)S(1)} async-done(((bf16[4,2,10240]{2,1,0:T(2,128)(2,1)}), bf16[4,2,10240]{2,1,0:T(2,128)(2,1)S(1)}, u32[]{:S(2)}, u32[]{:S(2)}) %all-to-all-start.1) | async-done | bytes 163872 | tf_op jit(solution)/shard_map/all_to_all | solution.py:34
  72.5 1.3 collective-permute-done
  73.8 0.2 copy.78
  74.0 4.5 %fusion.55 = (f32[16,8,8]{2,1,0:T(8,128)S(1)}, f32[16,8,8,128]{3,2,1,0:T(8,128)S(1)}) fusion(bf16[16,8,8,128]{3,2,1,0:T(8,128)(2,1)S(1)} %bitcast.154, pred[16,128]{1,0:T(8,128)(4,1)S(1)} %broadcast_compare_fusion, bf16[16,128,1024]{2,1,0:T(8,128)(2,1)} %param.10), kind=kOutput, calls=%fused_computation.83 | convolution fusion | flops 33946624 | bytes 4986880 | tf_op jit(solution)/shard_map/bkgd,btkd->bkgt/dot_general | solution.py:96
  78.7 0.4 fusion.16
  79.3 0.3 collective-permute-start.1
  79.5 3.4 %fusion.12 = f32[16,8,8,128]{3,2,1,0:T(8,128)S(1)} fusion(f32[16,8,8,128]{3,2,1,0:T(8,128)S(1)} %get-tuple-element.21, f32[16,8,8]{2,1,0:T(8,128)S(1)} %compare_select_fusion, f32[16,8,8]{2,1,0:T(8,128)S(1)} %get-tuple-element.20, pred[16,128]{1,0:T(8,128)(4,1)S(1)} %broadcast_compare_fusion, bf16[16,128,1024]{2,1,0:T(8,128)(2,1)} %param.11), kind=kOutput, calls=%fused_computation.8 | convolution fusion | flops 34078720 | bytes 5253120 | tf_op jit(solution)/shard_map/bkgt,btkd->bkgd/dot_general | solution.py:101
  83.3 0.5 collective-permute-start.2
  83.9 0.9 collective-permute-done.2
  84.8 0.3 fusion.24
  85.1 0.7 reduce.7
  85.8 0.8 reshape.208
  86.7 4.8 %all-to-all-start.2 = ((bf16[32,2,1088]{2,1,0:T(2,128)(2,1)}), bf16[32,2,1088]{2,1,0:T(2,128)(2,1)S(1)}, u32[]{:S(2)}, u32[]{:S(2)}) async-start(bf16[32,2,1088]{2,1,0:T(2,128)(2,1)} %reshape.208), calls=%async_computation.2 | async-start | bytes 294912 | tf_op jit(solution)/shard_map/all_to_all | solution.py:34
  91.5 4.1 %copy.100 = bf16[8192,128]{1,0:T(8,128)(2,1)} copy(bf16[8192,128]{0,1:T(8,128)(2,1)} %bitcast.151) | data formatting | bytes 4194304 | tf_op jit(solution)/shard_map/dot_general | solution.py:135
  95.7 0.2 reshape.196
  96.3 28.2 %all-to-all-done.2 = bf16[32,2,1088]{2,1,0:T(2,128)(2,1)S(1)} async-done(((bf16[32,2,1088]{2,1,0:T(2,128)(2,1)}), bf16[32,2,1088]{2,1,0:T(2,128)(2,1)S(1)}, u32[]{:S(2)}, u32[]{:S(2)}) %all-to-all-start.2) | async-done | bytes 139296 | tf_op jit(solution)/shard_map/all_to_all | solution.py:34
  124.6 0.7 copy.88
  125.5 0.2 fusion.51
  125.7 0.4 fusion.15
  126.0 2.3 %fusion.44 = f32[16,32,2,128]{3,0,2,1:T(8,128)S(1)} fusion(bf16[32,2,128,128]{3,2,1,0:T(8,128)(2,1)} %bitcast.148, f32[2048]{0:T(1024)S(1)} %fusion.15, f32[2048]{0:T(1024)S(1)} %squeeze.31, f32[16]{0:T(128)S(1)} %get-tuple-element.5, f32[16]{0:T(128)S(1)} %get-tuple-element.6), kind=kOutput, calls=%fused_computation.70 | convolution fusion | flops 33562624 | bytes 2637952 | tf_op jit(solution)/shard_map/dot_general | solution.py:135
  128.5 1.3 collective-permute-done.3
  129.9 35.2 %all_to_all.21 = bf16[32,16,128]{2,1,0:T(8,128)(2,1)S(1)} all-to-all(bf16[32,16,128]{2,1,0:T(8,128)(2,1)S(1)} %fusion.21), channel_id=1, replica_groups={{0,2,4,6,8,10,12,14,16,18,20,22,24,26,28,30,32,34,36,38,40,42,44,46,48,..., dimensions={0} | all-to-all | bytes 262144 | tf_op jit(solution)/shard_map/all_to_all | solution.py:34
  165.1 0.6 reduce_sum.55
  (55 shorter events, 2.5 us)
Async XLA Ops:
  0.0 1.6 copy-start
  0.0 72.4 %copy-start.1 = (s32[16]{0:T(128)S(1)}, s32[16]{0:T(128)}, u32[]{:S(2)}) copy-start(s32[16]{0:T(128)} %param.12) | copy-start | bytes 196
  62.1 9.9 %all-to-all-start.1 = ((bf16[4,2,10240]{2,1,0:T(2,128)(2,1)}), bf16[4,2,10240]{2,1,0:T(2,128)(2,1)S(1)}, u32[]{:S(2)}, u32[]{:S(2)}) async-start(bf16[4,2,10240]{2,1,0:T(2,128)(2,1)} %reshape.206), calls=%async_computation.1 | async-start | bytes 327680 | tf_op jit(solution)/shard_map/all_to_all | solution.py:34
  72.2 1.5 collective-permute-start
  79.3 4.6 %collective-permute-start.1 = (f32[32,16]{1,0:T(8,128)S(1)}, f32[32,16]{1,0:T(8,128)S(1)}, u32[]{:S(2)}, u32[]{:S(2)}) collective-permute-start(f32[32,16]{1,0:T(8,128)S(1)} %bitcast.166), channel_id=1, source_target_pairs={{0,1},{1,0},{2,3},{3,2},{4,5},{5,4},{6,7},{7,6},{8,9},{9,8},{10,11... | collective-permute-start | bytes 6152 | tf_op jit(solution)/shard_map/ppermute | solution.py:40
  83.3 1.5 collective-permute-start.2
  86.7 37.8 %all-to-all-start.2 = ((bf16[32,2,1088]{2,1,0:T(2,128)(2,1)}), bf16[32,2,1088]{2,1,0:T(2,128)(2,1)S(1)}, u32[]{:S(2)}, u32[]{:S(2)}) async-start(bf16[32,2,1088]{2,1,0:T(2,128)(2,1)} %reshape.208), calls=%async_computation.2 | async-start | bytes 294912 | tf_op jit(solution)/shard_map/all_to_all | solution.py:34
  128.4 1.5 collective-permute-start.3

commit v2 on v1

v2 whole, which is shorter than its diff:
```python
import math

import jax
import jax.numpy as jnp
from jax import lax
from jax.experimental import pallas as pl
from jax.experimental.pallas import tpu as pltpu
from jax.sharding import PartitionSpec as P

KV_HEADS = 8
HEAD_DIM = 128
CORES = 2
NEAR = 4
EMPTY = -1e30
PACK_ROWS = 24
STEP_ROWS = 2
INTERPRET = False


def same_core_groups(shards):
    return [[CORES * z + c for z in range(shards // CORES)] for c in range(CORES)]


def near_groups(shards):
    blocks = shards // CORES // NEAR
    return [
        [CORES * (NEAR * b + i) + c for i in range(NEAR)] for b in range(blocks) for c in range(CORES)
    ]


def far_groups(shards):
    blocks = shards // CORES // NEAR
    return [
        [CORES * (NEAR * b + i) + c for b in range(blocks)] for i in range(NEAR) for c in range(CORES)
    ]


def exchange(x, groups):
    return lax.all_to_all(
        x, "seq", split_axis=0, concat_axis=0, axis_index_groups=groups, tiled=True
    )


def to_partner(x, shards):
    return lax.ppermute(x, "seq", [(i, i ^ 1) for i in range(shards)])


def rounded(x):
    return lax.reduce_precision(x, exponent_bits=8, mantissa_bits=7)


def split_terms(x):
    high = rounded(x)
    middle = rounded(x - high)
    low = rounded(x - high - middle)
    return high.astype(jnp.bfloat16), middle.astype(jnp.bfloat16), low.astype(jnp.bfloat16)


def project_kernel(hidden_ref, w_query_ref, w_keyval_ref, packet_ref, acc_q, acc_kv):
    step = pl.program_id(0)

    @pl.when(step == 0)
    def _():
        acc_q[...] = jnp.zeros_like(acc_q)
        acc_kv[...] = jnp.zeros_like(acc_kv)

    hidden = hidden_ref[...]
    acc_q[...] += jnp.dot(hidden, w_query_ref[...], preferred_element_type=jnp.float32)
    acc_kv[...] += lax.dot_general(
        hidden, w_keyval_ref[...], (((1,), (1,)), ((), ())), preferred_element_type=jnp.float32
    )

    @pl.when(step == pl.num_programs(0) - 1)
    def _():
        batch, cols = acc_kv.shape
        rows = batch * cols // HEAD_DIM
        keyval = acc_kv[...]
        keyval = jnp.concatenate(
            [keyval[i * rows : (i + 1) * rows] for i in range(HEAD_DIM // cols)], axis=1
        )
        filler = jnp.zeros((PACK_ROWS - batch - rows, HEAD_DIM), jnp.float32)
        packet = jnp.concatenate([acc_q[...], keyval, filler], axis=0).astype(jnp.bfloat16)
        for copy in range(packet_ref.shape[0]):
            packet_ref[copy] = packet


def project(hidden_in, w_query, w_keyval_t, copies):
    batch, width = hidden_in.shape
    cols = w_keyval_t.shape[0]
    steps = 4
    chunk = width // steps
    return pl.pallas_call(
        project_kernel,
        grid=(steps,),
        in_specs=[
            pl.BlockSpec((batch, chunk), lambda k: (0, k)),
            pl.BlockSpec((chunk, HEAD_DIM), lambda k: (k, 0)),
            pl.BlockSpec((cols, chunk), lambda k: (0, k)),
        ],
        out_specs=pl.BlockSpec((copies, PACK_ROWS, HEAD_DIM), lambda k: (0, 0, 0)),
        out_shape=jax.ShapeDtypeStruct((copies, PACK_ROWS, HEAD_DIM), jnp.bfloat16),
        scratch_shapes=[
            pltpu.VMEM((batch, HEAD_DIM), jnp.float32),
            pltpu.VMEM((batch, cols), jnp.float32),
        ],
        interpret=INTERPRET,
        name="project",
    )(hidden_in, w_query, w_keyval_t)


def attend_kernel(lengths_ref, first_ref, own_ref, partner_ref, key_ref, value_ref,
                  mine_ref, theirs_ref, level_ref, q_scr, o_scr, level_scr):
    step = pl.program_id(0)
    blocks = own_ref.shape[0] // NEAR
    batch = mine_ref.shape[1]
    ctx_dev = key_ref.shape[1]
    group = CORES * NEAR
    f32, bf16 = jnp.float32, jnp.bfloat16

    @pl.when(step == 0)
    def _():
        for g in range(blocks):
            for c, ref in enumerate((own_ref, partner_ref)):
                for i in range(NEAR):
                    row = (g * group + c * NEAR + i) * batch
                    q_scr[row : row + batch, :] = ref[i * blocks + g, :batch, :].astype(f32)
        level_scr[...] = jnp.full(level_scr.shape, EMPTY, f32)

    lanes = lax.broadcasted_iota(jnp.int32, (group * blocks, ctx_dev), 1)
    level_lanes = lax.broadcasted_iota(jnp.int32, level_scr.shape, 1)
    for j in range(STEP_ROWS):
        b = step * STEP_ROWS + j
        used = lanes < lengths_ref[b] - first_ref[0]
        scores = []
        for g in range(blocks):
            query = q_scr[pl.ds(g * group * batch + b, group, stride=batch), :].astype(bf16)
            keys = key_ref[j, :, g * HEAD_DIM : (g + 1) * HEAD_DIM]
            scores.append(
                lax.dot_general(
                    query, keys, (((1,), (1,)), ((), ())), preferred_element_type=f32
                )
            )
        scores = jnp.concatenate(scores, axis=0) * (1.0 / math.sqrt(HEAD_DIM))
        scores = jnp.where(used, scores, EMPTY)
        top = jnp.max(scores, axis=1, keepdims=True)
        weights = jnp.where(used, jnp.exp(scores - top), 0.0)
        total = jnp.sum(weights, axis=1, keepdims=True)
        some = total > 0
        safe = jnp.where(some, total, 1.0)
        level = jnp.where(some, top + jnp.log(safe), EMPTY)
        level_scr[...] = jnp.where(level_lanes == b, level, level_scr[...])
        inverse = 1.0 / safe
        weights = weights.astype(bf16)
        for g in range(blocks):
            rows = slice(g * group, (g + 1) * group)
            values = value_ref[j, :, g * HEAD_DIM : (g + 1) * HEAD_DIM]
            out = jnp.dot(weights[rows], values, preferred_element_type=f32) * inverse[rows]
            o_scr[pl.ds(g * group * batch + b, group, stride=batch), :] = out

    @pl.when(step == pl.num_programs(0) - 1)
    def _():
        for g in range(blocks):
            for c, ref in enumerate((mine_ref, theirs_ref)):
                for i in range(NEAR):
                    row = (g * group + c * NEAR + i) * batch
                    ref[g * NEAR + i] = o_scr[row : row + batch, :].astype(bf16)
                start = c * NEAR * blocks + g * NEAR
                source = g * group + c * NEAR
                level_ref[start : start + NEAR, :] = level_scr[source : source + NEAR, :]


def attend(lengths, first, own, partner, key_cache, value_cache):
    batch, ctx_dev, width = key_cache.shape
    chips = own.shape[0]
    heads = CORES * chips
    whole = lambda *shape: pl.BlockSpec(shape, lambda s, *_: (0,) * len(shape))
    cache = pl.BlockSpec((STEP_ROWS, ctx_dev, width), lambda s, *_: (s, 0, 0))
    return pl.pallas_call(
        attend_kernel,
        grid_spec=pltpu.PrefetchScalarGridSpec(
            num_scalar_prefetch=2,
            grid=(batch // STEP_ROWS,),
            in_specs=[whole(*own.shape), whole(*partner.shape), cache, cache],
            out_specs=[
                whole(chips, batch, HEAD_DIM),
                whole(chips, batch, HEAD_DIM),
                whole(heads, HEAD_DIM),
            ],
            scratch_shapes=[
                pltpu.VMEM((heads * batch, HEAD_DIM), jnp.float32),
                pltpu.VMEM((heads * batch, HEAD_DIM), jnp.float32),
                pltpu.VMEM((heads, HEAD_DIM), jnp.float32),
            ],
        ),
        out_shape=[
            jax.ShapeDtypeStruct((chips, batch, HEAD_DIM), jnp.bfloat16),
            jax.ShapeDtypeStruct((chips, batch, HEAD_DIM), jnp.bfloat16),
            jax.ShapeDtypeStruct((heads, HEAD_DIM), jnp.float32),
        ],
        interpret=INTERPRET,
        name="attend",
    )(lengths, first, own, partner, key_cache, value_cache)


def body(hidden_in, w_query, w_keyval, key_cache, value_cache, lengths, w_out):
    batch, ctx_dev, half_width = key_cache.shape
    shards = lax.axis_size("seq")
    index = lax.axis_index("seq")
    core = index % CORES
    chips = shards // CORES
    blocks = chips // NEAR
    heads = w_out.shape[0] // HEAD_DIM * shards
    group = heads // KV_HEADS
    kv_cols = w_keyval.shape[1]
    f32, bf16 = jnp.float32, jnp.bfloat16

    w_cols = w_out.reshape(HEAD_DIM, chips, CORES, -1)
    w_first, w_second = w_cols[:, :, 0], w_cols[:, :, 1]
    w_mine = jnp.where(core == 0, w_first, w_second).reshape(HEAD_DIM, -1)
    w_theirs = jnp.where(core == 0, w_second, w_first).reshape(HEAD_DIM, -1)
    w_partner = to_partner(w_theirs, shards)

    packet = project(hidden_in, w_query, w_keyval.T, blocks)
    far = exchange(packet, far_groups(shards))
    near = exchange(
        jnp.broadcast_to(far[None], (NEAR, *far.shape)).reshape(chips, *far.shape[1:]),
        near_groups(shards),
    )
    partner = to_partner(near, shards)

    first = (index * ctx_dev).astype(jnp.int32)[None]
    mine, theirs, level = attend(lengths, first, near, partner, key_cache, value_cache)
    level = level[:, :batch]

    rows = batch * kv_cols // HEAD_DIM
    kv = jnp.stack([near[:, batch : batch + rows], partner[:, batch : batch + rows]])
    kv = jnp.where(core == 0, kv, kv[::-1]).reshape(CORES, NEAR, blocks, rows, HEAD_DIM)
    kv = kv.transpose(2, 1, 0, 3, 4).reshape(2, KV_HEADS, -1, rows, HEAD_DIM)
    own_kv = lax.dynamic_slice_in_dim(kv, index // group, 1, axis=1)[:, 0]
    own_kv = own_kv.reshape(2, HEAD_DIM // kv_cols, rows, -1, kv_cols).transpose(0, 3, 2, 1, 4)
    own_kv = own_kv.reshape(2, batch, HEAD_DIM).astype(f32)
    query_part = packet[0, :batch].astype(f32)
    score_new = jnp.sum(query_part * own_kv[0], axis=-1) / math.sqrt(HEAD_DIM)

    got_out = to_partner(theirs, shards).astype(f32)
    got_level = to_partner(level[chips:], shards)
    level = level[:chips]
    top = jnp.maximum(level, got_level)
    part_a = jnp.exp(level - top)
    part_b = jnp.exp(got_level - top)
    whole = part_a + part_b
    merged = mine.astype(f32) * (part_a / whole)[..., None] + got_out * (part_b / whole)[..., None]
    level = jnp.maximum(top + jnp.log(whole), EMPTY)
    stats = jnp.concatenate(split_terms(level), axis=1)
    stats = jnp.pad(stats, ((0, 0), (0, HEAD_DIM - stats.shape[1])))
    sent = jnp.concatenate([merged.astype(bf16).reshape(chips, -1), stats], axis=1)
    arrived = exchange(sent[:, None, :], same_core_groups(shards))[:, 0]
    q_size = batch * HEAD_DIM
    outs = arrived[:, :q_size].reshape(chips, batch, HEAD_DIM).astype(f32)
    levels = arrived[:, q_size : q_size + 3 * batch].astype(f32).reshape(chips, 3, batch)
    levels = levels[:, 0] + (levels[:, 1] + levels[:, 2])
    top = jnp.maximum(jnp.max(levels, axis=0), score_new)
    factor = jnp.exp(levels - top)
    factor_new = jnp.exp(score_new - top)
    numerator = jnp.sum(outs * factor[..., None], axis=0) + factor_new[:, None] * own_kv[1]
    denominator = jnp.sum(factor, axis=0) + factor_new
    attended = (numerator / denominator[:, None]).astype(bf16)

    attended_partner = to_partner(attended, shards)
    term = jnp.dot(attended, w_mine, preferred_element_type=f32) + jnp.dot(
        attended_partner, w_partner, preferred_element_type=f32
    )
    term = term.astype(bf16).reshape(batch, chips, -1).swapaxes(0, 1)
    arrived = exchange(term, same_core_groups(shards))
    return jnp.sum(arrived.astype(f32), axis=0).astype(bf16)


def solution(mesh):
    placed = (
        P("replica", None),
        P(None, "seq"),
        P(None, "seq"),
        P("replica", "seq", None),
        P("replica", "seq", None),
        P("replica"),
        P("seq", None),
    )
    return jax.shard_map(
        body, mesh=mesh, in_specs=placed, out_specs=P("replica", "seq"), check_vma=False
    )
```

time: 166 us -> 170 us (1.024)
  Pallas kernels: 0 us -> 14.2 us
  matrix products: 13 us -> 0.79 us
  blocking collectives: 90 us -> 101 us
  waiting for transfers between devices: 37.6 us -> 32.8 us
  starting transfers between devices: 9.72 us -> 5.8 us
    pallas_call x0 -> x2, Pallas kernels: none -> 14.2 us  [the longest x1 10.6 us: attend(): pl.pallas_call(attend_kernel, grid_spec=pltpu.PrefetchScalarGridSpec(num_...]
    dot_general x5 -> x2, matrix products: 13 us -> 0.79 us  [the longest x1 0.42 us: body(): jnp.dot(attended, w_mine, preferred_element_type=f32)]
    all_to_all x2 -> x3, blocking collectives: 90 us -> 101 us  [exchange(): lax.all_to_all(x, 'seq', split_axis=0, concat_axis=0, axis_index_groups=g...]
    all_to_all x2 -> x1, waiting for transfers between devices: 34.2 us -> 29.7 us  [exchange(): lax.all_to_all(x, 'seq', split_axis=0, concat_axis=0, axis_index_groups=g...]
    dot_general x1 -> x0, local copies, waits for them, and re-layouts: 4.11 us -> none  [body(): term = jnp.dot(attended, w_out, preferred_element_type=f32)]
    all_to_all x2 -> x1, starting transfers between devices: 8.68 us -> 4.77 us  [exchange(): lax.all_to_all(x, 'seq', split_axis=0, concat_axis=0, axis_index_groups=g...]
    another operation x0 -> x2, local copies, waits for them, and re-layouts: none -> 1.7 us  [body(): jnp.stack([near[:, batch:batch + rows], partner[:, batch:batch + rows]])]
    ppermute x4 -> x5, waiting for transfers between devices: 3.43 us -> 3.14 us  [to_partner(): return lax.ppermute(x, 'seq', [(i, i ^ 1) for i in range(shards)])]
  transfers between devices with their start and end apart: 6 -> 6, of which waited for: 5 -> 3; matrix products, arithmetic and copies ran while one was open for 5% -> 7% of each run, Pallas kernels for 0% -> 0%
where the time goes in v2:
time: 170 us; the launch traced here: 169 us
  blocking collectives  101 us (59%)
  waiting for transfers between devices  32.8 us (19%)
  Pallas kernels  14.2 us (8%)
  local copies, waits for them, and re-layouts  9.11 us (5%)
  starting transfers between devices  5.8 us (3%)
  other arithmetic  4.4 us (3%)
    all_to_all x3, blocking collectives, exchange(): lax.all_to_all(x, 'seq', split_axis=0, concat_axis=0, axis_index_groups=g...  101 us
    all_to_all x1, waiting for transfers between devices, exchange(): lax.all_to_all(x, 'seq', split_axis=0, concat_axis=0, axis_index_groups=g...  29.7 us
    pallas_call x1, Pallas kernels, attend(): pl.pallas_call(attend_kernel, grid_spec=pltpu.PrefetchScalarGridSpec(num_...  10.6 us
    unnamed x14, local copies, waits for them, and re-layouts  4.99 us
    all_to_all x1, starting transfers between devices, exchange(): lax.all_to_all(x, 'seq', split_axis=0, concat_axis=0, axis_index_groups=g...  4.77 us
    pallas_call x1, Pallas kernels, project(): pl.pallas_call(project_kernel, grid=(steps,), in_specs=[pl.BlockSpec((bat...  3.6 us
  transfers between devices with their start and end apart: 6, of which 3 were waited for; matrix products, arithmetic and copies ran while one was open for 7% of the time, Pallas kernels for 0%

profile of v2, /device:TPU:38, one launch (start us, length us, event | category | flops | bytes accessed | tf_op | source)
XLA Modules:
  0.0 168.7 jit_solution(16605060624842944153)
XLA Ops:
  0.0 3.6 %project.1 = bf16[8,24,128]{2,1,0:T(8,128)(2,1)} custom-call(bf16[16,8192]{1,0:T(8,128)(2,1)} %hidden_ref.1, bf16[8192,128]{1,0:T(8,128)(2,1)} %w_query_ref.1, bf16[32,8192]{1,0:T(8,128)(2,1)} %bitcast.82), custom_call_target="tpu_custom_call" | custom-call | tf_op jit(solution)/shard_map/project/pallas_call | solution.py:92
  3.6 55.6 %all_to_all.20 = bf16[8,24,128]{2,1,0:T(8,128)(2,1)S(1)} all-to-all(bf16[8,24,128]{2,1,0:T(8,128)(2,1)} %project.1), channel_id=1, replica_groups={{0,8,16,24,32,40,48,56},{1,9,17,25,33,41,49,57},{2,10,18,26,34,42,50,58..., dimensions={0} | all-to-all | bytes 98304 | tf_op jit(solution)/shard_map/all_to_all | solution.py:39
  59.2 10.5 %all_to_all.21.own_ref = bf16[32,24,128]{2,1,0:T(8,128)(2,1)S(1)} all-to-all(bf16[32,24,128]{2,1,0:T(8,128)(2,1)S(1)} %bitcast.78), channel_id=1, replica_groups={{0,2,4,6},{1,3,5,7},{8,10,12,14},{9,11,13,15},{16,18,20,22},{17,19,21,2..., dimensions={0} | all-to-all | bytes 393216 | tf_op jit(solution)/shard_map/all_to_all | solution.py:39
  69.8 3.3 %copy.39 = bf16[128,8192]{0,1:T(8,128)(2,1)S(1)} copy(bf16[128,8192]{1,0:T(8,128)(2,1)} %param.13) | data formatting | bytes 4194304 | tf_op args[6]
  73.1 0.7 copy-done.1
  73.8 10.6 %attend.1 = (bf16[32,16,128]{2,1,0:T(8,128)(2,1)}, bf16[32,16,128]{2,1,0:T(8,128)(2,1)}, f32[64,128]{1,0:T(8,128)}) custom-call(s32[16]{0:T(128)} %lengths_ref.1, s32[1]{0:T(128)} %bitcast.first_ref, bf16[32,24,128]{2,1,0:T(8,128)(2,1)} %copy-done, bf16[32,24,128]{2,1,0:T(8,128)(2,1)} %copy-done.1, bf16[16,128,1024]{2,1,0:T(8,128)(2,1)} %key_ref.1, ...), custom_call_target="tpu_custom_call" | custom-call | tf_op jit(solution)/shard_map/attend/pallas_call | solution.py:178
  84.3 0.7 slice.48
  85.1 0.4 collective-permute-start.1
  85.5 1.1 broadcast_select_fusion
  86.7 0.4 collective-permute-start.2
  87.3 2.4 %collective-permute-done.2 = bf16[32,16,128]{2,1,0:T(8,128)(2,1)S(1)} collective-permute-done((bf16[32,16,128]{2,1,0:T(8,128)(2,1)S(1)}, bf16[32,16,128]{2,1,0:T(8,128)(2,1)S(1)}, u32[]{:S(2)}, u32[]{:S(2)}) %collective-permute-start.2) | collective-permute-done | bytes 131104 | tf_op jit(solution)/shard_map/ppermute | solution.py:45
  89.7 0.2 add_convert_fusion
  90.0 0.5 broadcast.57
  90.5 0.7 reduce.3
  91.2 0.8 reshape.135
  92.0 4.8 %all-to-all-start.2 = ((bf16[32,2,1088]{2,1,0:T(2,128)(2,1)}), bf16[32,2,1088]{2,1,0:T(2,128)(2,1)S(1)}, u32[]{:S(2)}, u32[]{:S(2)}) async-start(bf16[32,2,1088]{2,1,0:T(2,128)(2,1)} %reshape.135), calls=%async_computation.2 | async-start | bytes 294912 | tf_op jit(solution)/shard_map/all_to_all | solution.py:39
  96.8 0.9 slice_bitcast_fusion.1
  97.6 0.9 slice_bitcast_fusion
  98.6 0.1 reshape.134
  99.0 0.8 fusion.11
  99.8 29.7 %all-to-all-done.2 = bf16[32,2,1088]{2,1,0:T(2,128)(2,1)S(1)} async-done(((bf16[32,2,1088]{2,1,0:T(2,128)(2,1)}), bf16[32,2,1088]{2,1,0:T(2,128)(2,1)S(1)}, u32[]{:S(2)}, u32[]{:S(2)}) %all-to-all-start.2) | async-done | bytes 139296 | tf_op jit(solution)/shard_map/all_to_all | solution.py:39
  129.5 0.1 reshape.136
  129.7 0.7 copy.35
  130.4 0.1 fusion.21
  130.6 0.2 fusion.23
  130.7 0.4 fusion.2
  131.2 0.1 collective-permute-start.3
  131.3 0.4 fusion.17
  131.7 0.7 collective-permute-done.3
  132.4 0.4 fusion.1
  132.8 35.3 %all_to_all.22 = bf16[32,16,128]{2,1,0:T(8,128)(2,1)S(1)} all-to-all(bf16[32,16,128]{2,1,0:T(8,128)(2,1)S(1)} %bitcast.81), channel_id=1, replica_groups={{0,2,4,6,8,10,12,14,16,18,20,22,24,26,28,30,32,34,36,38,40,42,44,46,48,..., dimensions={0} | all-to-all | bytes 262144 | tf_op jit(solution)/shard_map/all_to_all | solution.py:39
  168.1 0.6 reduce_sum.45
  (36 shorter events, 0.8 us)
Async XLA Ops:
  69.8 3.3 %copy-start = (bf16[32,24,128]{2,1,0:T(8,128)(2,1)}, bf16[32,24,128]{2,1,0:T(8,128)(2,1)S(1)}, u32[]{:S(2)}) copy-start(bf16[32,24,128]{2,1,0:T(8,128)(2,1)S(1)} %all_to_all.21.own_ref) | copy-start | bytes 589828
  69.8 3.3 %collective-permute-start = (bf16[32,24,128]{2,1,0:T(8,128)(2,1)S(1)}, bf16[32,24,128]{2,1,0:T(8,128)(2,1)S(1)}, u32[]{:S(2)}, u32[]{:S(2)}) collective-permute-start(bf16[32,24,128]{2,1,0:T(8,128)(2,1)S(1)} %all_to_all.21.own_ref), channel_id=1, source_target_pairs={{0,1},{1,0},{2,3},{3,2},{4,5},{5,4},{6,7},{7,6},{8,9},{9,8},{10,11... | collective-permute-start | bytes 589832 | tf_op jit(solution)/shard_map/ppermute | solution.py:45
  73.1 0.7 copy-start.1
  85.1 2.1 %collective-permute-start.1 = (f32[32,16]{1,0:T(8,128)S(1)}, f32[32,16]{1,0:T(8,128)S(1)}, u32[]{:S(2)}, u32[]{:S(2)}) collective-permute-start(f32[32,16]{1,0:T(8,128)S(1)} %slice.48), channel_id=1, source_target_pairs={{0,1},{1,0},{2,3},{3,2},{4,5},{5,4},{6,7},{7,6},{8,9},{9,8},{10,11... | collective-permute-start | bytes 6152 | tf_op jit(solution)/shard_map/ppermute | solution.py:45
  85.5 1.2 copy-start.4
  85.5 1.6 copy-start.3
  85.5 4.2 %copy-start.2 = (bf16[32,16,128]{2,1,0:T(8,128)(2,1)S(1)}, bf16[32,16,128]{2,1,0:T(8,128)(2,1)}, u32[]{:S(2)}) copy-start(bf16[32,16,128]{2,1,0:T(8,128)(2,1)} %get-tuple-element.8) | copy-start | bytes 393220
  86.6 45.1 %collective-permute-start.4 = (bf16[128,4096]{0,1:T(8,128)(2,1)}, bf16[128,4096]{0,1:T(8,128)(2,1)S(1)}, u32[]{:S(2)}, u32[]{:S(2)}) collective-permute-start(bf16[128,4096]{0,1:T(8,128)(2,1)} %bitcast.22), channel_id=1, source_target_pairs={{0,1},{1,0},{2,3},{3,2},{4,5},{5,4},{6,7},{7,6},{8,9},{9,8},{10,11... | collective-permute-start | bytes 3145736 | tf_op jit(solution)/shard_map/ppermute | solution.py:45
  86.7 3.0 %collective-permute-start.2 = (bf16[32,16,128]{2,1,0:T(8,128)(2,1)S(1)}, bf16[32,16,128]{2,1,0:T(8,128)(2,1)S(1)}, u32[]{:S(2)}, u32[]{:S(2)}) collective-permute-start(bf16[32,16,128]{2,1,0:T(8,128)(2,1)S(1)} %copy-done.4), channel_id=1, source_target_pairs={{0,1},{1,0},{2,3},{3,2},{4,5},{5,4},{6,7},{7,6},{8,9},{9,8},{10,11... | collective-permute-start | bytes 393224 | tf_op jit(solution)/shard_map/ppermute | solution.py:45
  92.0 37.5 %all-to-all-start.2 = ((bf16[32,2,1088]{2,1,0:T(2,128)(2,1)}), bf16[32,2,1088]{2,1,0:T(2,128)(2,1)S(1)}, u32[]{:S(2)}, u32[]{:S(2)}) async-start(bf16[32,2,1088]{2,1,0:T(2,128)(2,1)} %reshape.135), calls=%async_computation.2 | async-start | bytes 294912 | tf_op jit(solution)/shard_map/all_to_all | solution.py:39
  131.2 1.2 collective-permute-start.3

commit v3 on v2

v3 whole, which is shorter than its diff:
```python
import math

import jax
import jax.numpy as jnp
from jax import lax
from jax.experimental import pallas as pl
from jax.experimental.pallas import tpu as pltpu
from jax.sharding import PartitionSpec as P

KV_HEADS = 8
HEAD_DIM = 128
CORES = 2
NEAR = 4
EMPTY = -1e30
PACK_ROWS = 24
STEP_ROWS = 4
INTERPRET = False


def same_core_groups(shards):
    return [[CORES * z + c for z in range(shards // CORES)] for c in range(CORES)]


def near_groups(shards):
    blocks = shards // CORES // NEAR
    return [
        [CORES * (NEAR * b + i) + c for i in range(NEAR)] for b in range(blocks) for c in range(CORES)
    ]


def far_groups(shards):
    blocks = shards // CORES // NEAR
    return [
        [CORES * (NEAR * b + i) + c for b in range(blocks)] for i in range(NEAR) for c in range(CORES)
    ]


def exchange(x, groups):
    return lax.all_to_all(
        x, "seq", split_axis=0, concat_axis=0, axis_index_groups=groups, tiled=True
    )


def to_partner(x, shards):
    return lax.ppermute(x, "seq", [(i, i ^ 1) for i in range(shards)])


def rounded(x):
    return lax.reduce_precision(x, exponent_bits=8, mantissa_bits=7)


def split_terms(x):
    high = rounded(x)
    middle = rounded(x - high)
    low = rounded(x - high - middle)
    return high.astype(jnp.bfloat16), middle.astype(jnp.bfloat16), low.astype(jnp.bfloat16)


def in_vmem(x):
    return x if INTERPRET else pltpu.with_memory_space_constraint(x, pltpu.VMEM)


def in_hbm(x):
    return x if INTERPRET else pltpu.with_memory_space_constraint(x, pltpu.HBM)


def vmem_out(shape, dtype):
    return jax.ShapeDtypeStruct(shape, dtype) if INTERPRET else pltpu.VMEM(shape, dtype)


def hbm_out(shape, dtype):
    return jax.ShapeDtypeStruct(shape, dtype) if INTERPRET else pltpu.HBM(shape, dtype)


def whole():
    return pl.BlockSpec(memory_space=pltpu.VMEM)


def limit(mib):
    return pltpu.CompilerParams(vmem_limit_bytes=mib << 20)


def project_kernel(hidden_ref, w_query_ref, w_keyval_ref, packet_ref, acc_q, acc_kv):
    step = pl.program_id(0)

    @pl.when(step == 0)
    def _():
        acc_q[...] = jnp.zeros_like(acc_q)
        acc_kv[...] = jnp.zeros_like(acc_kv)

    hidden = hidden_ref[...]
    acc_q[...] += jnp.dot(hidden, w_query_ref[...], preferred_element_type=jnp.float32)
    acc_kv[...] += lax.dot_general(
        hidden, w_keyval_ref[...], (((1,), (1,)), ((), ())), preferred_element_type=jnp.float32
    )

    @pl.when(step == pl.num_programs(0) - 1)
    def _():
        batch, cols = acc_kv.shape
        rows = batch * cols // HEAD_DIM
        keyval = acc_kv[...]
        keyval = jnp.concatenate(
            [keyval[i * rows : (i + 1) * rows] for i in range(HEAD_DIM // cols)], axis=1
        )
        filler = jnp.zeros((PACK_ROWS - batch - rows, HEAD_DIM), jnp.float32)
        packet = jnp.concatenate([acc_q[...], keyval, filler], axis=0).astype(jnp.bfloat16)
        for copy in range(packet_ref.shape[0]):
            packet_ref[copy] = packet


def project(hidden_in, w_query, w_keyval_t, copies):
    batch, width = hidden_in.shape
    cols = w_keyval_t.shape[0]
    steps = 2
    chunk = width // steps
    return pl.pallas_call(
        project_kernel,
        grid=(steps,),
        in_specs=[
            pl.BlockSpec((batch, chunk), lambda k: (0, k)),
            pl.BlockSpec((chunk, HEAD_DIM), lambda k: (k, 0)),
            pl.BlockSpec((cols, chunk), lambda k: (0, k)),
        ],
        out_specs=whole(),
        out_shape=vmem_out((copies, PACK_ROWS, HEAD_DIM), jnp.bfloat16),
        scratch_shapes=[
            pltpu.VMEM((batch, HEAD_DIM), jnp.float32),
            pltpu.VMEM((batch, cols), jnp.float32),
        ],
        compiler_params=limit(8),
        interpret=INTERPRET,
        name="project",
    )(in_hbm(hidden_in), in_hbm(w_query), in_hbm(w_keyval_t))


def transpose_keys_kernel(key_ref, out_ref):
    for j in range(key_ref.shape[0]):
        for g in range(key_ref.shape[2] // HEAD_DIM):
            columns = slice(g * HEAD_DIM, (g + 1) * HEAD_DIM)
            out_ref[j, columns, :] = key_ref[j, :, columns].T


def transpose_keys(key_cache):
    batch, ctx_dev, width = key_cache.shape
    rows = 2
    return pl.pallas_call(
        transpose_keys_kernel,
        grid=(batch // rows,),
        in_specs=[pl.BlockSpec((rows, ctx_dev, width), lambda s: (s, 0, 0))],
        out_specs=pl.BlockSpec((rows, width, ctx_dev), lambda s: (s, 0, 0)),
        out_shape=hbm_out((batch, width, ctx_dev), key_cache.dtype),
        compiler_params=limit(8),
        interpret=INTERPRET,
        name="transpose_keys",
    )(in_hbm(key_cache))


def attend_kernel(lengths_ref, first_ref, own_ref, partner_ref, key_ref, value_ref,
                  mine_ref, theirs_ref, level_ref, level_theirs_ref, q_scr, o_scr, level_scr,
                  keys_scr, values_scr, sems):
    step = pl.program_id(0)
    blocks = own_ref.shape[0] // NEAR
    batch = mine_ref.shape[1]
    ctx_dev = value_ref.shape[1]
    group = CORES * NEAR
    f32, bf16 = jnp.float32, jnp.bfloat16

    def copies(part):
        rows = pl.ds(part * STEP_ROWS, STEP_ROWS)
        return (
            pltpu.make_async_copy(key_ref.at[rows], keys_scr.at[rows], sems.at[0, part]),
            pltpu.make_async_copy(value_ref.at[rows], values_scr.at[rows], sems.at[1, part]),
        )

    @pl.when(step == 0)
    def _():
        for part in range(batch // STEP_ROWS):
            for copy in copies(part):
                copy.start()
        for g in range(blocks):
            for c, ref in enumerate((own_ref, partner_ref)):
                for i in range(NEAR):
                    row = (g * group + c * NEAR + i) * batch
                    q_scr[row : row + batch, :] = ref[i * blocks + g, :batch, :].astype(f32)
        level_scr[...] = jnp.full(level_scr.shape, EMPTY, f32)

    for copy in copies(step):
        copy.wait()
    lanes = lax.broadcasted_iota(jnp.int32, (group * blocks, ctx_dev), 1)
    level_lanes = lax.broadcasted_iota(jnp.int32, level_scr.shape, 1)
    step_scores = []
    for j in range(STEP_ROWS):
        b = step * STEP_ROWS + j
        scores = []
        for g in range(blocks):
            query = q_scr[pl.ds(g * group * batch + b, group, stride=batch), :].astype(bf16)
            keys = keys_scr[b, g * HEAD_DIM : (g + 1) * HEAD_DIM, :]
            scores.append(jnp.dot(query, keys, preferred_element_type=f32))
        step_scores.append(jnp.concatenate(scores, axis=0) * (1.0 / math.sqrt(HEAD_DIM)))
    step_weights, step_inverse = [], []
    levels = level_scr[...]
    for j in range(STEP_ROWS):
        b = step * STEP_ROWS + j
        used = lanes < lengths_ref[b] - first_ref[0]
        scores = jnp.where(used, step_scores[j], EMPTY)
        top = jnp.max(scores, axis=1, keepdims=True)
        weights = jnp.where(used, jnp.exp(scores - top), 0.0)
        total = jnp.sum(weights, axis=1, keepdims=True)
        some = total > 0
        safe = jnp.where(some, total, 1.0)
        level = jnp.where(some, top + jnp.log(safe), EMPTY)
        levels = jnp.where(level_lanes == b, level, levels)
        step_inverse.append(1.0 / safe)
        step_weights.append(weights.astype(bf16))
    level_scr[...] = levels
    outs = []
    for j in range(STEP_ROWS):
        b = step * STEP_ROWS + j
        for g in range(blocks):
            rows = slice(g * group, (g + 1) * group)
            values = values_scr[b, :, g * HEAD_DIM : (g + 1) * HEAD_DIM]
            out = jnp.dot(step_weights[j][rows], values, preferred_element_type=f32)
            outs.append(out * step_inverse[j][rows])
    for j in range(STEP_ROWS):
        b = step * STEP_ROWS + j
        for g in range(blocks):
            o_scr[pl.ds(g * group * batch + b, group, stride=batch), :] = outs[j * blocks + g]

    @pl.when(step == pl.num_programs(0) - 1)
    def _():
        for g in range(blocks):
            halves = ((mine_ref, level_ref), (theirs_ref, level_theirs_ref))
            for c, (ref, level) in enumerate(halves):
                for i in range(NEAR):
                    row = (g * group + c * NEAR + i) * batch
                    ref[g * NEAR + i] = o_scr[row : row + batch, :].astype(bf16)
                source = g * group + c * NEAR
                level[g * NEAR : (g + 1) * NEAR, :] = level_scr[source : source + NEAR, :]


def attend(lengths, first, own, partner, keys, values):
    batch = keys.shape[0]
    chips = own.shape[0]
    heads = CORES * chips
    return pl.pallas_call(
        attend_kernel,
        grid_spec=pltpu.PrefetchScalarGridSpec(
            num_scalar_prefetch=2,
            grid=(batch // STEP_ROWS,),
            in_specs=[whole(), whole()] + [pl.BlockSpec(memory_space=pl.ANY)] * 2,
            out_specs=[whole()] * 4,
            scratch_shapes=[
                pltpu.VMEM((heads * batch, HEAD_DIM), jnp.float32),
                pltpu.VMEM((heads * batch, HEAD_DIM), jnp.float32),
                pltpu.VMEM((heads, HEAD_DIM), jnp.float32),
                pltpu.VMEM(keys.shape, keys.dtype),
                pltpu.VMEM(values.shape, values.dtype),
                pltpu.SemaphoreType.DMA((2, batch // STEP_ROWS)),
            ],
        ),
        out_shape=[
            vmem_out((chips, batch, HEAD_DIM), jnp.bfloat16),
            vmem_out((chips, batch, HEAD_DIM), jnp.bfloat16),
            vmem_out((chips, HEAD_DIM), jnp.float32),
            vmem_out((chips, HEAD_DIM), jnp.float32),
        ],
        compiler_params=limit(16),
        interpret=INTERPRET,
        name="attend",
    )(lengths, first, in_vmem(own), in_vmem(partner), in_hbm(keys), in_hbm(values))


def sort_columns_kernel(core_ref, w_ref, mine_ref, theirs_ref):
    swap = core_ref[0] == 1
    for i in range(w_ref.shape[1] // (CORES * HEAD_DIM)):
        first = w_ref[:, CORES * i * HEAD_DIM : (CORES * i + 1) * HEAD_DIM]
        second = w_ref[:, (CORES * i + 1) * HEAD_DIM : (CORES * i + 2) * HEAD_DIM]
        columns = slice(i * HEAD_DIM, (i + 1) * HEAD_DIM)
        mine_ref[:, columns] = jnp.where(swap, second, first)
        theirs_ref[:, columns] = jnp.where(swap, first, second)


def sort_columns(core, w_out):
    rows, width = w_out.shape
    steps = 4
    chunk = width // steps
    half = pl.BlockSpec((rows, chunk // CORES), lambda s, *_: (0, s))
    return pl.pallas_call(
        sort_columns_kernel,
        grid_spec=pltpu.PrefetchScalarGridSpec(
            num_scalar_prefetch=1,
            grid=(steps,),
            in_specs=[pl.BlockSpec((rows, chunk), lambda s, *_: (0, s))],
            out_specs=[half, half],
        ),
        out_shape=[jax.ShapeDtypeStruct((rows, width // CORES), w_out.dtype)] * 2,
        compiler_params=limit(8),
        interpret=INTERPRET,
        name="sort_columns",
    )(core, w_out)


def output_kernel(own_ref, partner_ref, w_own_ref, w_partner_ref, out_ref):
    blocks = out_ref.shape[1]
    for z in range(NEAR * blocks):
        columns = slice(z * HEAD_DIM, (z + 1) * HEAD_DIM)
        term = jnp.dot(own_ref[...], w_own_ref[:, columns], preferred_element_type=jnp.float32)
        term += jnp.dot(
            partner_ref[...], w_partner_ref[:, columns], preferred_element_type=jnp.float32
        )
        out_ref[z % NEAR, z // NEAR] = term.astype(out_ref.dtype)


def output_terms(own, partner, w_own, w_partner):
    batch = own.shape[0]
    blocks = w_own.shape[1] // HEAD_DIM // NEAR
    return pl.pallas_call(
        output_kernel,
        in_specs=[whole()] * 4,
        out_specs=whole(),
        out_shape=vmem_out((NEAR, blocks, batch, HEAD_DIM), jnp.bfloat16),
        compiler_params=limit(8),
        interpret=INTERPRET,
        name="output_terms",
    )(in_vmem(own), in_vmem(partner), in_vmem(w_own), in_vmem(w_partner))


def body(hidden_in, w_query, w_keyval, key_cache, value_cache, lengths, w_out):
    batch, ctx_dev, half_width = key_cache.shape
    shards = lax.axis_size("seq")
    index = lax.axis_index("seq")
    core = index % CORES
    chips = shards // CORES
    blocks = chips // NEAR
    heads = w_out.shape[0] // HEAD_DIM * shards
    group = heads // KV_HEADS
    kv_cols = w_keyval.shape[1]
    f32, bf16 = jnp.float32, jnp.bfloat16

    first = (index * ctx_dev).astype(jnp.int32)[None]
    own_group = index // group
    hidden_in, first, core, own_group = lax.optimization_barrier(
        (hidden_in, first, core, own_group)
    )

    packet = project(hidden_in, w_query, w_keyval.T, blocks)
    packet, keys = lax.optimization_barrier((packet, key_cache))
    far = exchange(packet, far_groups(shards))
    keys = transpose_keys(keys)
    far, keys = lax.optimization_barrier((far, keys))
    near = exchange(
        jnp.broadcast_to(far[None], (NEAR, *far.shape)).reshape(chips, *far.shape[1:]),
        near_groups(shards),
    )
    partner = to_partner(near, shards)

    mine, theirs, level, level_theirs = attend(
        lengths, first, near, partner, keys, value_cache
    )

    rows = batch * kv_cols // HEAD_DIM
    kv = jnp.stack([near[:, batch : batch + rows], partner[:, batch : batch + rows]])
    kv = jnp.where(core == 0, kv, kv[::-1]).reshape(CORES, NEAR, blocks, rows, HEAD_DIM)
    kv = kv.transpose(2, 1, 0, 3, 4).reshape(2, KV_HEADS, -1, rows, HEAD_DIM)
    own_kv = lax.dynamic_slice_in_dim(kv, own_group, 1, axis=1)[:, 0]
    own_kv = own_kv.reshape(2, HEAD_DIM // kv_cols, rows, -1, kv_cols).transpose(0, 3, 2, 1, 4)
    own_kv = own_kv.reshape(2, batch, HEAD_DIM).astype(f32)
    query_part = packet[0, :batch].astype(f32)
    score_new = jnp.sum(query_part * own_kv[0], axis=-1) / math.sqrt(HEAD_DIM)

    got_out = to_partner(theirs, shards).astype(f32)
    got_level = to_partner(level_theirs, shards)[:, :batch]
    level = level[:, :batch]
    top = jnp.maximum(level, got_level)
    part_a = jnp.exp(level - top)
    part_b = jnp.exp(got_level - top)
    whole = part_a + part_b
    merged = mine.astype(f32) * (part_a / whole)[..., None] + got_out * (part_b / whole)[..., None]
    level = jnp.maximum(top + jnp.log(whole), EMPTY)
    stats = jnp.concatenate(split_terms(level), axis=1)
    stats = jnp.pad(stats, ((0, 0), (0, HEAD_DIM - stats.shape[1])))
    sent = jnp.concatenate([merged.astype(bf16).reshape(chips, -1), stats], axis=1)
    sent, w_now = lax.optimization_barrier((sent, w_out))
    arrived = exchange(sent[:, None, :], same_core_groups(shards))[:, 0]

    w_mine, w_theirs = sort_columns(core.astype(jnp.int32)[None], w_now)
    w_partner = to_partner(w_theirs, shards)
    q_size = batch * HEAD_DIM
    outs = arrived[:, :q_size].reshape(chips, batch, HEAD_DIM).astype(f32)
    levels = arrived[:, q_size : q_size + 3 * batch].astype(f32).reshape(chips, 3, batch)
    levels = levels[:, 0] + (levels[:, 1] + levels[:, 2])
    top = jnp.maximum(jnp.max(levels, axis=0), score_new)
    factor = jnp.exp(levels - top)
    factor_new = jnp.exp(score_new - top)
    numerator = jnp.sum(outs * factor[..., None], axis=0) + factor_new[:, None] * own_kv[1]
    denominator = jnp.sum(factor, axis=0) + factor_new
    attended = (numerator / denominator[:, None]).astype(bf16)

    attended_partner = to_partner(attended, shards)
    term = output_terms(attended, attended_partner, w_mine, w_partner)
    arrived = exchange(term.reshape(chips, batch, -1), near_groups(shards))
    term = jnp.sum(arrived.reshape(NEAR, blocks, batch, -1).astype(f32), axis=0).astype(bf16)
    arrived = exchange(term, far_groups(shards))
    return jnp.sum(arrived.astype(f32), axis=0).astype(bf16)


def solution(mesh):
    placed = (
        P("replica", None),
        P(None, "seq"),
        P(None, "seq"),
        P("replica", "seq", None),
        P("replica", "seq", None),
        P("replica"),
        P("seq", None),
    )
    return jax.shard_map(
        body, mesh=mesh, in_specs=placed, out_specs=P("replica", "seq"), check_vma=False
    )
```

time: 170 us -> 157 us (0.924)
  blocking collectives: 101 us -> 44.8 us
  starting transfers between devices: 5.8 us -> 38.6 us
  waiting for transfers between devices: 32.8 us -> 49.6 us
  local copies, waits for them, and re-layouts: 9.11 us -> 2.65 us
  Pallas kernels: 14.2 us -> 17.6 us
    all_to_all x3, blocking collectives: 101 us -> 44.8 us  [exchange(): lax.all_to_all(x, 'seq', split_axis=0, concat_axis=0, axis_index_groups=g...]
    all_to_all x1 -> x2, starting transfers between devices: 4.77 us -> 37.8 us  [exchange(): lax.all_to_all(x, 'seq', split_axis=0, concat_axis=0, axis_index_groups=g...]
    all_to_all x1 -> x2, waiting for transfers between devices: 29.7 us -> 46.1 us  [exchange(): lax.all_to_all(x, 'seq', split_axis=0, concat_axis=0, axis_index_groups=g...]
    pallas_call x0 -> x3, Pallas kernels: none -> 9.9 us  [the longest x1 7.22 us: transpose_keys(): pl.pallas_call(transpose_keys_kernel, grid=(batch // rows,), in_specs=[pl...]
    pallas_call x1, Pallas kernels: 10.6 us -> 4.94 us  [attend(): pl.pallas_call(attend_kernel, grid_spec=pltpu.PrefetchScalarGridSpec(num_...]
    unnamed x14 -> x7, local copies, waits for them, and re-layouts: 4.99 us -> 1.03 us
  transfers between devices with their start and end apart: 6 -> 7, of which waited for: 3 -> 6; matrix products, arithmetic and copies ran while one was open for 7% -> 2% of each run, Pallas kernels for 0% -> 6%
where the time goes in v3:
time: 157 us
  waiting for transfers between devices  49.6 us (32%)
  blocking collectives  44.8 us (29%)
  starting transfers between devices  38.6 us (25%)
  Pallas kernels  17.6 us (11%)
  other arithmetic  3.28 us (2%)
  local copies, waits for them, and re-layouts  2.65 us (2%)
    all_to_all x2, waiting for transfers between devices, exchange(): lax.all_to_all(x, 'seq', split_axis=0, concat_axis=0, axis_index_groups=g...  46.1 us
    all_to_all x3, blocking collectives, exchange(): lax.all_to_all(x, 'seq', split_axis=0, concat_axis=0, axis_index_groups=g...  44.8 us
    all_to_all x2, starting transfers between devices, exchange(): lax.all_to_all(x, 'seq', split_axis=0, concat_axis=0, axis_index_groups=g...  37.8 us
    pallas_call x1, Pallas kernels, transpose_keys(): pl.pallas_call(transpose_keys_kernel, grid=(batch // rows,), in_specs=[pl...  7.22 us
    pallas_call x1, Pallas kernels, attend(): pl.pallas_call(attend_kernel, grid_spec=pltpu.PrefetchScalarGridSpec(num_...  4.94 us
    ppermute x5, waiting for transfers between devices, to_partner(): return lax.ppermute(x, 'seq', [(i, i ^ 1) for i in range(shards)])  3.44 us
  transfers between devices with their start and end apart: 7, of which 6 were waited for; matrix products, arithmetic and copies ran while one was open for 2% of the time, Pallas kernels for 6%

profile of v3, /device:TPU:38, one launch (start us, length us, event | category | flops | bytes accessed | tf_op | source)
XLA Modules:
  0.0 156.7 jit_solution(16841046964403559596)
XLA Ops:
  0.0 2.8 %project.1 = bf16[8,24,128]{2,1,0:T(8,128)(2,1)} custom-call(bf16[16,8192]{1,0:T(8,128)(2,1)} %hidden_ref, bf16[8192,128]{1,0:T(8,128)(2,1)} %w_query_ref.1, bf16[32,8192]{1,0:T(8,128)(2,1)} %bitcast.49), custom_call_target="tpu_custom_call" | custom-call | tf_op jit(solution)/shard_map/project/pallas_call | solution.py:116
  2.8 31.6 %all-to-all-start = ((bf16[8,24,128]{2,1,0:T(8,128)(2,1)}), bf16[8,24,128]{2,1,0:T(8,128)(2,1)S(1)}, u32[]{:S(2)}, u32[]{:S(2)}) async-start(bf16[8,24,128]{2,1,0:T(8,128)(2,1)} %project.1), calls=%async_computation | async-start | bytes 98304 | tf_op jit(solution)/shard_map/all_to_all | solution.py:39
  34.4 7.2 %transpose_keys.1.key_ref = bf16[16,1024,128]{2,1,0:T(8,128)(2,1)} custom-call(bf16[16,128,1024]{2,1,0:T(8,128)(2,1)} %key_ref), custom_call_target="tpu_custom_call" | custom-call | tf_op jit(solution)/shard_map/transpose_keys/pallas_call | solution.py:146
  41.6 16.8 %all-to-all-done = bf16[8,24,128]{2,1,0:T(8,128)(2,1)S(1)} async-done(((bf16[8,24,128]{2,1,0:T(8,128)(2,1)}), bf16[8,24,128]{2,1,0:T(8,128)(2,1)S(1)}, u32[]{:S(2)}, u32[]{:S(2)}) %all-to-all-start) | async-done | bytes 49184 | tf_op jit(solution)/shard_map/all_to_all | solution.py:39
  58.4 10.5 %all_to_all.25.own_ref = bf16[32,24,128]{2,1,0:T(8,128)(2,1)S(1)} all-to-all(bf16[32,24,128]{2,1,0:T(8,128)(2,1)S(1)} %bitcast.44), channel_id=1, replica_groups={{0,2,4,6},{1,3,5,7},{8,10,12,14},{9,11,13,15},{16,18,20,22},{17,19,21,2..., dimensions={0} | all-to-all | bytes 393216 | tf_op jit(solution)/shard_map/all_to_all | solution.py:39
  68.9 1.4 collective-permute-done.partner_ref
  70.4 4.9 %attend.1 = (bf16[32,16,128]{2,1,0:T(8,128)(2,1)S(1)}, bf16[32,16,128]{2,1,0:T(8,128)(2,1)S(1)}, f32[32,128]{1,0:T(8,128)S(1)}, f32[32,128]{1,0:T(8,128)S(1)}) custom-call(s32[16]{0:T(128)S(1)} %copy-done.1, s32[1]{0:T(128)} %bitcast.first_ref, bf16[32,24,128]{2,1,0:T(8,128)(2,1)S(1)} %all_to_all.25.own_ref, ...), custom_call_target="tpu_custom_call" | custom-call | tf_op jit(solution)/shard_map/attend/pallas_call | solution.py:245
  75.3 0.3 collective-permute-start.1
  75.6 0.4 collective-permute-start.2
  76.0 0.7 collective-permute-done.1
  76.8 0.2 collective-permute-done.2
  77.0 0.2 add_convert_fusion
  77.2 0.5 broadcast.44
  77.7 0.7 reduce.4
  78.4 0.8 reshape.103
  79.3 6.2 %all-to-all-start.2 = ((bf16[32,2,1088]{2,1,0:T(2,128)(2,1)}), bf16[32,2,1088]{2,1,0:T(2,128)(2,1)S(1)}, u32[]{:S(2)}, u32[]{:S(2)}) async-start(bf16[32,2,1088]{2,1,0:T(2,128)(2,1)} %reshape.103), calls=%async_computation.2 | async-start | bytes 294912 | tf_op jit(solution)/shard_map/all_to_all | solution.py:39
  85.7 0.1 reshape.102
  85.8 0.1 squeeze.14
  85.9 2.0 %sort_columns.1 = (bf16[128,4096]{1,0:T(8,128)(2,1)S(1)}, bf16[128,4096]{1,0:T(8,128)(2,1)}) custom-call(s32[1]{0:T(128)} %bitcast.17.core_ref, bf16[128,8192]{1,0:T(8,128)(2,1)S(1)} %copy-done), custom_call_target="tpu_custom_call" | custom-call | tf_op jit(solution)/shard_map/sort_columns/pallas_call | solution.py:288
  88.0 0.8 fusion.9
  88.8 0.1 squeeze.15
  88.9 29.3 %all-to-all-done.2 = bf16[32,2,1088]{2,1,0:T(2,128)(2,1)S(1)} async-done(((bf16[32,2,1088]{2,1,0:T(2,128)(2,1)}), bf16[32,2,1088]{2,1,0:T(2,128)(2,1)S(1)}, u32[]{:S(2)}, u32[]{:S(2)}) %all-to-all-start.2) | async-done | bytes 139296 | tf_op jit(solution)/shard_map/all_to_all | solution.py:39
  118.2 0.1 reshape.104
  118.4 0.7 copy.28
  119.1 0.1 fusion.13
  119.3 0.2 fusion.15
  119.5 0.4 fusion
  120.0 1.1 collective-permute-done.3.partner_ref
  121.1 0.6 output_terms.1
  121.8 8.9 %all_to_all.26 = bf16[32,16,128]{2,1,0:T(8,128)(2,1)S(1)} all-to-all(bf16[32,16,128]{2,1,0:T(8,128)(2,1)S(1)} %bitcast.41), channel_id=1, replica_groups={{0,2,4,6},{1,3,5,7},{8,10,12,14},{9,11,13,15},{16,18,20,22},{17,19,21,2..., dimensions={0} | all-to-all | bytes 262144 | tf_op jit(solution)/shard_map/all_to_all | solution.py:39
  130.7 25.4 %all_to_all.27 = bf16[8,16,128]{2,1,0:T(8,128)(2,1)S(1)} all-to-all(bf16[8,16,128]{2,1,0:T(8,128)(2,1)S(1)} %reduce_sum.57), channel_id=1, replica_groups={{0,8,16,24,32,40,48,56},{1,9,17,25,33,41,49,57},{2,10,18,26,34,42,50,58..., dimensions={0} | all-to-all | bytes 65536 | tf_op jit(solution)/shard_map/all_to_all | solution.py:39
  156.1 0.6 reduce_sum.58
  (29 shorter events, 0.7 us)
Async XLA Ops:
  2.8 55.6 %all-to-all-start = ((bf16[8,24,128]{2,1,0:T(8,128)(2,1)}), bf16[8,24,128]{2,1,0:T(8,128)(2,1)S(1)}, u32[]{:S(2)}, u32[]{:S(2)}) async-start(bf16[8,24,128]{2,1,0:T(8,128)(2,1)} %project.1), calls=%async_computation | async-start | bytes 98304 | tf_op jit(solution)/shard_map/all_to_all | solution.py:39
  34.4 36.0 %copy-start.1 = (s32[16]{0:T(128)S(1)}, s32[16]{0:T(128)}, u32[]{:S(2)}) copy-start(s32[16]{0:T(128)} %lengths_ref.1) | copy-start | bytes 196
  68.9 17.0 %copy-start = (bf16[128,8192]{1,0:T(8,128)(2,1)S(1)}, bf16[128,8192]{1,0:T(8,128)(2,1)}, u32[]{:S(2)}) copy-start(bf16[128,8192]{1,0:T(8,128)(2,1)} %w_ref) | copy-start | bytes 6291460
  68.9 1.4 collective-permute-start
  75.3 1.3 collective-permute-start.1
  75.6 1.4 collective-permute-start.2
  79.3 39.0 %all-to-all-start.2 = ((bf16[32,2,1088]{2,1,0:T(2,128)(2,1)}), bf16[32,2,1088]{2,1,0:T(2,128)(2,1)S(1)}, u32[]{:S(2)}, u32[]{:S(2)}) async-start(bf16[32,2,1088]{2,1,0:T(2,128)(2,1)} %reshape.103), calls=%async_computation.2 | async-start | bytes 294912 | tf_op jit(solution)/shard_map/all_to_all | solution.py:39
  87.9 32.1 %collective-permute-start.4 = (bf16[128,4096]{1,0:T(8,128)(2,1)}, bf16[128,4096]{1,0:T(8,128)(2,1)S(1)}, u32[]{:S(2)}, u32[]{:S(2)}) collective-permute-start(bf16[128,4096]{1,0:T(8,128)(2,1)} %get-tuple-element.36), channel_id=1, source_target_pairs={{0,1},{1,0},{2,3},{3,2},{4,5},{5,4},{6,7},{7,6},{8,9},{9,8},{10,11... | collective-permute-start | bytes 3145736 | tf_op jit(solution)/shard_map/ppermute | solution.py:45
  119.9 1.2 collective-permute-start.3

commit v4 on v3

--- a/solution.py
+++ b/solution.py
@@ -1,3 +1,4 @@
+import functools
 import math
 
 import jax
@@ -6,6 +7,7 @@
 from jax.experimental import pallas as pl
 from jax.experimental.pallas import tpu as pltpu
 from jax.sharding import PartitionSpec as P
+
 
 KV_HEADS = 8
 HEAD_DIM = 128
@@ -17,10 +19,6 @@
 INTERPRET = False
 
 
-def same_core_groups(shards):
-    return [[CORES * z + c for z in range(shards // CORES)] for c in range(CORES)]
-
-
 def near_groups(shards):
     blocks = shards // CORES // NEAR
     return [
@@ -43,17 +41,6 @@
 
 def to_partner(x, shards):
     return lax.ppermute(x, "seq", [(i, i ^ 1) for i in range(shards)])
-
-
-def rounded(x):
-    return lax.reduce_precision(x, exponent_bits=8, mantissa_bits=7)
-
-
-def split_terms(x):
-    high = rounded(x)
-    middle = rounded(x - high)
-    low = rounded(x - high - middle)
-    return high.astype(jnp.bfloat16), middle.astype(jnp.bfloat16), low.astype(jnp.bfloat16)
 
 
 def in_vmem(x):
@@ -229,13 +216,14 @@
     @pl.when(step == pl.num_programs(0) - 1)
     def _():
         for g in range(blocks):
-            halves = ((mine_ref, level_ref), (theirs_ref, level_theirs_ref))
-            for c, (ref, level) in enumerate(halves):
+            for c, ref in enumerate((mine_ref, theirs_ref)):
                 for i in range(NEAR):
                     row = (g * group + c * NEAR + i) * batch
-                    ref[g * NEAR + i] = o_scr[row : row + batch, :].astype(bf16)
-                source = g * group + c * NEAR
-                level[g * NEAR : (g + 1) * NEAR, :] = level_scr[source : source + NEAR, :]
+                    ref[i * blocks + g] = o_scr[row : row + batch, :].astype(bf16)
+        for c, level in enumerate((level_ref, level_theirs_ref)):
+            for i in range(NEAR):
+                rows = level_scr[pl.ds(c * NEAR + i, blocks, stride=group), :]
+                level[i * blocks : (i + 1) * blocks, :] = rows
 
 
 def attend(lengths, first, own, partner, keys, values):
@@ -270,6 +258,166 @@
     )(lengths, first, in_vmem(own), in_vmem(partner), in_hbm(keys), in_hbm(values))
 
 
+def as_columns(*parts):
+    count = sum(part.shape[0] for part in parts)
+    filler = jnp.zeros((HEAD_DIM - count, HEAD_DIM), jnp.float32)
+    return jnp.concatenate([*parts, filler], axis=0).T
+
+
+def write_packet(ref, at, out, level):
+    row = lax.broadcasted_iota(jnp.int32, (PACK_ROWS - out.shape[0], HEAD_DIM), 0)
+    high = level.astype(jnp.bfloat16).astype(jnp.float32)
+    middle = (level - high).astype(jnp.bfloat16).astype(jnp.float32)
+    low = level - high - middle
+    stats = jnp.where(row == 0, high, jnp.where(row == 1, middle, jnp.where(row == 2, low, 0.0)))
+    ref[at] = jnp.concatenate([out, stats], axis=0).astype(jnp.bfloat16)
+
+
+def read_levels(ref, batch, scr):
+    for r in range(ref.shape[0]):
+        stats = ref[r, batch:, :].astype(jnp.float32)
+        scr[r : r + 1, :] = stats[0:1] + (stats[1:2] + stats[2:3])
+    return scr[...]
+
+
+def merge_cores_kernel(mine_ref, level_ref, got_ref, got_level_ref, out_ref):
+    batch = mine_ref.shape[1]
+    count = mine_ref.shape[0]
+    level, got = level_ref[...], got_level_ref[...]
+    top = jnp.maximum(level, got)
+    part_a, part_b = jnp.exp(level - top), jnp.exp(got - top)
+    total = part_a + part_b
+    merged = top + jnp.log(total)
+    columns = as_columns(part_a / total, part_b / total)
+    for r in range(count):
+        out = mine_ref[r].astype(jnp.float32) * columns[:batch, r : r + 1]
+        out += got_ref[r].astype(jnp.float32) * columns[:batch, count + r : count + r + 1]
+        write_packet(out_ref, r, out, merged[r : r + 1, :])
+
+
+def merge_cores(mine, level, got, got_level):
+    chips, _, _ = mine.shape
+    return pl.pallas_call(
+        merge_cores_kernel,
+        in_specs=[whole()] * 4,
+        out_specs=whole(),
+        out_shape=vmem_out((chips, PACK_ROWS, HEAD_DIM), jnp.bfloat16),
+        compiler_params=limit(8),
+        interpret=INTERPRET,
+        name="merge_cores",
+    )(in_vmem(mine), in_vmem(level), in_vmem(got), in_vmem(got_level))
+
+
+def merge_near_kernel(batch, packet_ref, out_ref, level_scr):
+    blocks = out_ref.shape[0]
+    levels = read_levels(packet_ref, batch, level_scr)
+    parts = [levels[i * blocks : (i + 1) * blocks] for i in range(NEAR)]
+    top = functools.reduce(jnp.maximum, parts)
+    parts = [jnp.exp(part - top) for part in parts]
+    total = functools.reduce(jnp.add, parts)
+    merged = top + jnp.log(total)
+    columns = as_columns(*[part / total for part in parts])
+    for k in range(blocks):
+        out = 0.0
+        for i in range(NEAR):
+            r = i * blocks + k
+            rows = packet_ref[r, :batch, :].astype(jnp.float32)
+            out += rows * columns[:batch, r : r + 1]
+        write_packet(out_ref, k, out, merged[k : k + 1, :])
+
+
+def merge_near(packets, batch):
+    count = packets.shape[0]
+    return pl.pallas_call(
+        functools.partial(merge_near_kernel, batch),
+        in_specs=[whole()],
+        out_specs=whole(),
+        out_shape=vmem_out((count // NEAR, PACK_ROWS, HEAD_DIM), jnp.bfloat16),
+        scratch_shapes=[pltpu.VMEM((count, HEAD_DIM), jnp.float32)],
+        compiler_params=limit(8),
+        interpret=INTERPRET,
+        name="merge_near",
+    )(in_vmem(packets))
+
+
+def merge_far_kernel(packet_ref, score_ref, value_ref, out_ref, level_scr):
+    batch = out_ref.shape[0]
+    count = packet_ref.shape[0]
+    levels = read_levels(packet_ref, batch, level_scr)
+    score = score_ref[...]
+    top = jnp.maximum(jnp.max(levels, axis=0, keepdims=True), score)
+    parts, part_new = jnp.exp(levels - top), jnp.exp(score - top)
+    total = jnp.sum(parts, axis=0, keepdims=True) + part_new
+    columns = as_columns(parts / total, part_new / total)
+    out = value_ref[...] * columns[:batch, count : count + 1]
+    for r in range(count):
+        out += packet_ref[r, :batch, :].astype(jnp.float32) * columns[:batch, r : r + 1]
+    out_ref[...] = out.astype(out_ref.dtype)
+
+
+def merge_far(packets, score_new, value_new):
+    count = packets.shape[0]
+    batch = value_new.shape[0]
+    return pl.pallas_call(
+        merge_far_kernel,
+        in_specs=[whole()] * 3,
+        out_specs=whole(),
+        out_shape=vmem_out((batch, HEAD_DIM), jnp.bfloat16),
+        scratch_shapes=[pltpu.VMEM((count, HEAD_DIM), jnp.float32)],
+        compiler_params=limit(8),
+        interpret=INTERPRET,
+        name="merge_far",
+    )(in_vmem(packets), in_vmem(score_new), in_vmem(value_new))
+
+
+def new_token_kernel(where_ref, query_ref, own_ref, partner_ref, score_ref, value_ref):
+    core, own_group = where_ref[0], where_ref[1]
+    batch = value_ref.shape[0]
+    blocks = own_ref.shape[0] // NEAR
+    group_chips = own_ref.shape[0] // (2 * KV_HEADS)
+    rows_of = []
+    for half in range(2):
+        pieces = []
+        for e in range(group_chips):
+            chip = (half * KV_HEADS + own_group) * group_chips + e
+            at = chip % NEAR * blocks + chip // NEAR
+            own = own_ref[at, batch:, :].astype(jnp.float32)
+            partner = partner_ref[at, batch:, :].astype(jnp.float32)
+            pieces += [jnp.where(core == 0, own, partner), jnp.where(core == 0, partner, own)]
+        cols = HEAD_DIM // len(pieces)
+        rows = batch * cols // HEAD_DIM
+        parts = []
+        for q in range(HEAD_DIM // cols):
+            lanes = slice(q * cols, (q + 1) * cols)
+            parts.append(jnp.concatenate([piece[:rows, lanes] for piece in pieces], axis=1))
+        rows_of.append(jnp.concatenate(parts, axis=0))
+    query = query_ref[0, :batch, :].astype(jnp.float32)
+    score = jnp.sum(query * rows_of[0], axis=1, keepdims=True) * (1.0 / math.sqrt(HEAD_DIM))
+    row = lax.broadcasted_iota(jnp.int32, (batch, HEAD_DIM), 0)
+    lane = lax.broadcasted_iota(jnp.int32, (batch, HEAD_DIM), 1)
+    score_ref[...] = jnp.sum(jnp.where(row == lane, score, 0.0), axis=0, keepdims=True)
+    value_ref[...] = rows_of[1]
+
+
+def new_token(where, packet, own, partner, batch):
+    return pl.pallas_call(
+        new_token_kernel,
+        grid_spec=pltpu.PrefetchScalarGridSpec(
+            num_scalar_prefetch=1,
+            grid=(1,),
+            in_specs=[whole()] * 3,
+            out_specs=[whole()] * 2,
+        ),
+        out_shape=[
+            vmem_out((1, HEAD_DIM), jnp.float32),
+            vmem_out((batch, HEAD_DIM), jnp.float32),
+        ],
+        compiler_params=limit(8),
+        interpret=INTERPRET,
+        name="new_token",
+    )(where, in_vmem(packet), in_vmem(own), in_vmem(partner))
+
+
 def sort_columns_kernel(core_ref, w_ref, mine_ref, theirs_ref):
     swap = core_ref[0] == 1
     for i in range(w_ref.shape[1] // (CORES * HEAD_DIM)):
@@ -325,8 +473,8 @@
     )(in_vmem(own), in_vmem(partner), in_vmem(w_own), in_vmem(w_partner))
 
 
-def body(hidden_in, w_query, w_keyval, key_cache, value_cache, lengths, w_out):
-    batch, ctx_dev, half_width = key_cache.shape
+def layer(hidden_in, w_query, w_keyval, key_cache, value_cache, lengths, w_out):
+    batch, ctx_dev, _ = key_cache.shape
     shards = lax.axis_size("seq")
     index = lax.axis_index("seq")
     core = index % CORES
@@ -334,14 +482,11 @@
     blocks = chips // NEAR
     heads = w_out.shape[0] // HEAD_DIM * shards
     group = heads // KV_HEADS
-    kv_cols = w_keyval.shape[1]
     f32, bf16 = jnp.float32, jnp.bfloat16
 
     first = (index * ctx_dev).astype(jnp.int32)[None]
-    own_group = index // group
-    hidden_in, first, core, own_group = lax.optimization_barrier(
-        (hidden_in, first, core, own_group)
-    )
+    where = jnp.stack([core, index // group]).astype(jnp.int32)
+    hidden_in, first, where = lax.optimization_barrier((hidden_in, first, where))
 
     packet = project(hidden_in, w_query, w_keyval.T, blocks)
     packet, keys = lax.optimization_barrier((packet, key_cache))
@@ -358,43 +503,16 @@
         lengths, first, near, partner, keys, value_cache
     )
 
-    rows = batch * kv_cols // HEAD_DIM
-    kv = jnp.stack([near[:, batch : batch + rows], partner[:, batch : batch + rows]])
-    kv = jnp.where(core == 0, kv, kv[::-1]).reshape(CORES, NEAR, blocks, rows, HEAD_DIM)
-    kv = kv.transpose(2, 1, 0, 3, 4).reshape(2, KV_HEADS, -1, rows, HEAD_DIM)
-    own_kv = lax.dynamic_slice_in_dim(kv, own_group, 1, axis=1)[:, 0]
-    own_kv = own_kv.reshape(2, HEAD_DIM // kv_cols, rows, -1, kv_cols).transpose(0, 3, 2, 1, 4)
-    own_kv = own_kv.reshape(2, batch, HEAD_DIM).astype(f32)
-    query_part = packet[0, :batch].astype(f32)
-    score_new = jnp.sum(query_part * own_kv[0], axis=-1) / math.sqrt(HEAD_DIM)
-
-    got_out = to_partner(theirs, shards).astype(f32)
-    got_level = to_partner(level_theirs, shards)[:, :batch]
-    level = level[:, :batch]
-    top = jnp.maximum(level, got_level)
-    part_a = jnp.exp(level - top)
-    part_b = jnp.exp(got_level - top)
-    whole = part_a + part_b
-    merged = mine.astype(f32) * (part_a / whole)[..., None] + got_out * (part_b / whole)[..., None]
-    level = jnp.maximum(top + jnp.log(whole), EMPTY)
-    stats = jnp.concatenate(split_terms(level), axis=1)
-    stats = jnp.pad(stats, ((0, 0), (0, HEAD_DIM - stats.shape[1])))
-    sent = jnp.concatenate([merged.astype(bf16).reshape(chips, -1), stats], axis=1)
-    sent, w_now = lax.optimization_barrier((sent, w_out))
-    arrived = exchange(sent[:, None, :], same_core_groups(shards))[:, 0]
-
-    w_mine, w_theirs = sort_columns(core.astype(jnp.int32)[None], w_now)
+    got = to_partner(theirs, shards)
+    got_level = to_partner(level_theirs, shards)
+    packets = exchange(merge_cores(mine, level, got, got_level), near_groups(shards))
+    packets = merge_near(packets, batch)
+    packets = exchange(packets, far_groups(shards))
+
+    score_new, value_new = new_token(where, packet, near, partner, batch)
+    w_mine, w_theirs = sort_columns(where, w_out)
     w_partner = to_partner(w_theirs, shards)
-    q_size = batch * HEAD_DIM
-    outs = arrived[:, :q_size].reshape(chips, batch, HEAD_DIM).astype(f32)
-    levels = arrived[:, q_size : q_size + 3 * batch].astype(f32).reshape(chips, 3, batch)
-    levels = levels[:, 0] + (levels[:, 1] + levels[:, 2])
-    top = jnp.maximum(jnp.max(levels, axis=0), score_new)
-    factor = jnp.exp(levels - top)
-    factor_new = jnp.exp(score_new - top)
-    numerator = jnp.sum(outs * factor[..., None], axis=0) + factor_new[:, None] * own_kv[1]
-    denominator = jnp.sum(factor, axis=0) + factor_new
-    attended = (numerator / denominator[:, None]).astype(bf16)
+    attended = merge_far(packets, score_new, value_new)
 
     attended_partner = to_partner(attended, shards)
     term = output_terms(attended, attended_partner, w_mine, w_partner)
@@ -415,5 +533,5 @@
         P("seq", None),
     )
     return jax.shard_map(
-        body, mesh=mesh, in_specs=placed, out_specs=P("replica", "seq"), check_vma=False
+        layer, mesh=mesh, in_specs=placed, out_specs=P("replica", "seq"), check_vma=False
     )

time: 157 us -> 156 us (level)
  Pallas kernels: 17.6 us -> 21.9 us
  waiting for transfers between devices: 49.6 us -> 45.6 us
  starting transfers between devices: 38.6 us -> 41.2 us
  other arithmetic: 3.28 us -> 0.7 us
  local copies, waits for them, and re-layouts: 2.65 us -> 0.96 us
    all_to_all x2 -> x3, waiting for transfers between devices: 46.1 us -> 42.2 us  [exchange(): lax.all_to_all(x, 'seq', split_axis=0, concat_axis=0, axis_index_groups=g...]
    pallas_call x0 -> x4, Pallas kernels: none -> 3.7 us  [the longest x1 1.5 us: new_token(): pl.pallas_call(new_token_kernel, grid_spec=pltpu.PrefetchScalarGridSpec(n...]
    all_to_all x2 -> x3, starting transfers between devices: 37.8 us -> 40.1 us  [exchange(): lax.all_to_all(x, 'seq', split_axis=0, concat_axis=0, axis_index_groups=g...]
  transfers between devices with their start and end apart: 7 -> 8, of which waited for: 6 -> 6; matrix products, arithmetic and copies ran while one was open for 2% -> 0% of each run, Pallas kernels for 6% -> 8%
where the time goes in v4:
time: 156 us; the launch traced here: 155 us
  waiting for transfers between devices  45.6 us (29%)
  blocking collectives  44.8 us (29%)
  starting transfers between devices  41.2 us (26%)
  Pallas kernels  21.9 us (14%)
    all_to_all x3, blocking collectives, exchange(): lax.all_to_all(x, 'seq', split_axis=0, concat_axis=0, axis_index_groups=g...  44.8 us
    all_to_all x3, waiting for transfers between devices, exchange(): lax.all_to_all(x, 'seq', split_axis=0, concat_axis=0, axis_index_groups=g...  42.2 us
    all_to_all x3, starting transfers between devices, exchange(): lax.all_to_all(x, 'seq', split_axis=0, concat_axis=0, axis_index_groups=g...  40.1 us
    pallas_call x1, Pallas kernels, transpose_keys(): pl.pallas_call(transpose_keys_kernel, grid=(batch // rows,), in_specs=[pl...  7.2 us
    pallas_call x1, Pallas kernels, attend(): pl.pallas_call(attend_kernel, grid_spec=pltpu.PrefetchScalarGridSpec(num_...  4.94 us
    ppermute x5, waiting for transfers between devices, to_partner(): return lax.ppermute(x, 'seq', [(i, i ^ 1) for i in range(shards)])  3.43 us
  transfers between devices with their start and end apart: 8, of which 6 were waited for; matrix products, arithmetic and copies ran while one was open for 0% of the time, Pallas kernels for 8%

profile of v4, /device:TPU:38, one launch (start us, length us, event | category | flops | bytes accessed | tf_op | source)
XLA Modules:
  0.0 155.3 jit_solution(1603204623042955435)
XLA Ops:
  0.0 0.1 pad_add_fusion.where_ref.core_ref
  0.1 2.8 %project.1.query_ref = bf16[8,24,128]{2,1,0:T(8,128)(2,1)} custom-call(bf16[16,8192]{1,0:T(8,128)(2,1)} %hidden_ref, bf16[8192,128]{1,0:T(8,128)(2,1)} %w_query_ref.1, bf16[32,8192]{1,0:T(8,128)(2,1)} %bitcast.10), custom_call_target="tpu_custom_call" | custom-call | tf_op jit(solution)/shard_map/project/pallas_call | solution.py:103
  2.8 31.6 %all-to-all-start = ((bf16[8,24,128]{2,1,0:T(8,128)(2,1)}), bf16[8,24,128]{2,1,0:T(8,128)(2,1)S(1)}, u32[]{:S(2)}, u32[]{:S(2)}) async-start(bf16[8,24,128]{2,1,0:T(8,128)(2,1)} %project.1.query_ref), calls=%async_computation | async-start | bytes 98304 | tf_op jit(solution)/shard_map/all_to_all | solution.py:37
  34.4 7.2 %transpose_keys.1.key_ref = bf16[16,1024,128]{2,1,0:T(8,128)(2,1)} custom-call(bf16[16,128,1024]{2,1,0:T(8,128)(2,1)} %key_ref), custom_call_target="tpu_custom_call" | custom-call | tf_op jit(solution)/shard_map/transpose_keys/pallas_call | solution.py:133
  41.6 16.8 %all-to-all-done = bf16[8,24,128]{2,1,0:T(8,128)(2,1)S(1)} async-done(((bf16[8,24,128]{2,1,0:T(8,128)(2,1)}), bf16[8,24,128]{2,1,0:T(8,128)(2,1)S(1)}, u32[]{:S(2)}, u32[]{:S(2)}) %all-to-all-start) | async-done | bytes 49184 | tf_op jit(solution)/shard_map/all_to_all | solution.py:37
  58.5 10.5 %all_to_all.30.own_ref = bf16[32,24,128]{2,1,0:T(8,128)(2,1)S(1)} all-to-all(bf16[32,24,128]{2,1,0:T(8,128)(2,1)S(1)} %bitcast.8), channel_id=1, replica_groups={{0,2,4,6},{1,3,5,7},{8,10,12,14},{9,11,13,15},{16,18,20,22},{17,19,21,2..., dimensions={0} | all-to-all | bytes 393216 | tf_op jit(solution)/shard_map/all_to_all | solution.py:37
  69.0 0.0 collective-permute-start
  69.0 1.4 collective-permute-done.partner_ref
  70.4 0.0 copy-done.3
  70.5 4.9 %attend.1 = (bf16[32,16,128]{2,1,0:T(8,128)(2,1)S(1)}, bf16[32,16,128]{2,1,0:T(8,128)(2,1)S(1)}, f32[32,128]{1,0:T(8,128)S(1)}, f32[32,128]{1,0:T(8,128)S(1)}) custom-call(s32[16]{0:T(128)S(1)} %copy-done.3, s32[1]{0:T(128)} %bitcast.first_ref, bf16[32,24,128]{2,1,0:T(8,128)(2,1)S(1)} %all_to_all.30.own_ref, ...), custom_call_target="tpu_custom_call" | custom-call | tf_op jit(solution)/shard_map/attend/pallas_call | solution.py:233
  75.4 0.3 collective-permute-start.1
  75.7 0.4 collective-permute-start.2
  76.0 0.9 collective-permute-done.2.got_level_ref
  76.9 0.0 collective-permute-done.1.got_ref
  76.9 1.1 merge_cores.1
  78.0 3.5 %all-to-all-start.2 = ((bf16[32,24,128]{2,1,0:T(8,128)(2,1)}), bf16[32,24,128]{2,1,0:T(8,128)(2,1)S(1)}, u32[]{:S(2)}, u32[]{:S(2)}) async-start(bf16[32,24,128]{2,1,0:T(8,128)(2,1)} %merge_cores.1), calls=%async_computation.2 | async-start | bytes 393216 | tf_op jit(solution)/shard_map/all_to_all | solution.py:37
  81.5 2.6 %sort_columns.1 = (bf16[128,4096]{1,0:T(8,128)(2,1)S(1)}, bf16[128,4096]{1,0:T(8,128)(2,1)}) custom-call(s32[2]{0:T(128)S(1)} %pad_add_fusion.where_ref.core_ref, bf16[128,8192]{1,0:T(8,128)(2,1)S(1)} %copy-done), custom_call_target="tpu_custom_call" | custom-call | tf_op jit(solution)/shard_map/sort_columns/pallas_call | solution.py:436
  84.1 0.3 collective-permute-start.4
  84.4 5.2 %all-to-all-done.2.packet_ref = bf16[32,24,128]{2,1,0:T(8,128)(2,1)S(1)} async-done(((bf16[32,24,128]{2,1,0:T(8,128)(2,1)}), bf16[32,24,128]{2,1,0:T(8,128)(2,1)S(1)}, u32[]{:S(2)}, u32[]{:S(2)}) %all-to-all-start.2) | async-done | bytes 196640 | tf_op jit(solution)/shard_map/all_to_all | solution.py:37
  89.6 0.9 merge_near.1
  90.5 5.1 %all-to-all-start.3 = ((bf16[8,24,128]{2,1,0:T(8,128)(2,1)}), bf16[8,24,128]{2,1,0:T(8,128)(2,1)S(1)}, u32[]{:S(2)}, u32[]{:S(2)}) async-start(bf16[8,24,128]{2,1,0:T(8,128)(2,1)} %merge_near.1), calls=%async_computation.3 | async-start | bytes 98304 | tf_op jit(solution)/shard_map/all_to_all | solution.py:37
  95.6 0.9 copy-done.2
  96.5 1.5 new_token.1
  98.0 20.2 %all-to-all-done.3.packet_ref = bf16[8,24,128]{2,1,0:T(8,128)(2,1)S(1)} async-done(((bf16[8,24,128]{2,1,0:T(8,128)(2,1)}), bf16[8,24,128]{2,1,0:T(8,128)(2,1)S(1)}, u32[]{:S(2)}, u32[]{:S(2)}) %all-to-all-start.3) | async-done | bytes 49184 | tf_op jit(solution)/shard_map/all_to_all | solution.py:37
  118.2 0.2 merge_far.1.own_ref
  118.4 0.1 collective-permute-start.3
  118.6 0.0 collective-permute-done.4.w_partner_ref
  118.6 1.1 collective-permute-done.3.partner_ref
  119.7 0.6 output_terms.1
  120.4 9.2 %all_to_all.31 = bf16[32,16,128]{2,1,0:T(8,128)(2,1)S(1)} all-to-all(bf16[32,16,128]{2,1,0:T(8,128)(2,1)S(1)} %bitcast.7), channel_id=1, replica_groups={{0,2,4,6},{1,3,5,7},{8,10,12,14},{9,11,13,15},{16,18,20,22},{17,19,21,2..., dimensions={0} | all-to-all | bytes 262144 | tf_op jit(solution)/shard_map/all_to_all | solution.py:37
  129.6 25.1 %all_to_all.32 = bf16[8,16,128]{2,1,0:T(8,128)(2,1)S(1)} all-to-all(bf16[8,16,128]{2,1,0:T(8,128)(2,1)S(1)} %reduce_sum.24), channel_id=1, replica_groups={{0,8,16,24,32,40,48,56},{1,9,17,25,33,41,49,57},{2,10,18,26,34,42,50,58..., dimensions={0} | all-to-all | bytes 65536 | tf_op jit(solution)/shard_map/all_to_all | solution.py:37
  154.7 0.6 reduce_sum.25
  (8 shorter events, 0.1 us)
Async XLA Ops:
  2.8 55.6 %all-to-all-start = ((bf16[8,24,128]{2,1,0:T(8,128)(2,1)}), bf16[8,24,128]{2,1,0:T(8,128)(2,1)S(1)}, u32[]{:S(2)}, u32[]{:S(2)}) async-start(bf16[8,24,128]{2,1,0:T(8,128)(2,1)} %project.1.query_ref), calls=%async_computation | async-start | bytes 98304 | tf_op jit(solution)/shard_map/all_to_all | solution.py:37
  34.4 36.0 %copy-start.3 = (s32[16]{0:T(128)S(1)}, s32[16]{0:T(128)}, u32[]{:S(2)}) copy-start(s32[16]{0:T(128)} %lengths_ref.1) | copy-start | bytes 196
  69.0 12.4 %copy-start = (bf16[128,8192]{1,0:T(8,128)(2,1)S(1)}, bf16[128,8192]{1,0:T(8,128)(2,1)}, u32[]{:S(2)}) copy-start(bf16[128,8192]{1,0:T(8,128)(2,1)} %w_ref.1) | copy-start | bytes 6291460
  69.0 1.4 collective-permute-start
  70.4 5.0 %copy-start.1 = (bf16[32,24,128]{2,1,0:T(8,128)(2,1)}, bf16[32,24,128]{2,1,0:T(8,128)(2,1)S(1)}, u32[]{:S(2)}) copy-start(bf16[32,24,128]{2,1,0:T(8,128)(2,1)S(1)} %collective-permute-done.partner_ref) | copy-start | bytes 589828
  75.4 1.5 collective-permute-start.1
  75.7 1.2 collective-permute-start.2
  78.0 11.6 %all-to-all-start.2 = ((bf16[32,24,128]{2,1,0:T(8,128)(2,1)}), bf16[32,24,128]{2,1,0:T(8,128)(2,1)S(1)}, u32[]{:S(2)}, u32[]{:S(2)}) async-start(bf16[32,24,128]{2,1,0:T(8,128)(2,1)} %merge_cores.1), calls=%async_computation.2 | async-start | bytes 393216 | tf_op jit(solution)/shard_map/all_to_all | solution.py:37
  84.1 34.5 %collective-permute-start.4 = (bf16[128,4096]{1,0:T(8,128)(2,1)}, bf16[128,4096]{1,0:T(8,128)(2,1)S(1)}, u32[]{:S(2)}, u32[]{:S(2)}) collective-permute-start(bf16[128,4096]{1,0:T(8,128)(2,1)} %get-tuple-element.34), channel_id=1, source_target_pairs={{0,1},{1,0},{2,3},{3,2},{4,5},{5,4},{6,7},{7,6},{8,9},{9,8},{10,11... | collective-permute-start | bytes 3145736 | tf_op jit(solution)/shard_map/ppermute | solution.py:43
  90.5 27.7 %all-to-all-start.3 = ((bf16[8,24,128]{2,1,0:T(8,128)(2,1)}), bf16[8,24,128]{2,1,0:T(8,128)(2,1)S(1)}, u32[]{:S(2)}, u32[]{:S(2)}) async-start(bf16[8,24,128]{2,1,0:T(8,128)(2,1)} %merge_near.1), calls=%async_computation.3 | async-start | bytes 98304 | tf_op jit(solution)/shard_map/all_to_all | solution.py:37
  95.6 0.9 copy-start.2
  118.4 1.3 collective-permute-start.3

commit v5 on v4

v5 whole, which is shorter than its diff:
```python
import functools
import math

import jax
import jax.numpy as jnp
from jax import lax
from jax.experimental import pallas as pl
from jax.experimental.pallas import tpu as pltpu
from jax.sharding import PartitionSpec as P


KV_HEADS = 8
HEAD_DIM = 128
CORES = 2
NEAR = 4
EMPTY = -1e30
PACK_ROWS = 24
STEP_ROWS = 4
INTERPRET = False


def near_groups(shards):
    blocks = shards // CORES // NEAR
    return [
        [CORES * (NEAR * b + i) + c for i in range(NEAR)] for b in range(blocks) for c in range(CORES)
    ]


def far_groups(shards):
    blocks = shards // CORES // NEAR
    return [
        [CORES * (NEAR * b + i) + c for b in range(blocks)] for i in range(NEAR) for c in range(CORES)
    ]


def exchange(x, groups):
    return lax.all_to_all(
        x, "seq", split_axis=0, concat_axis=0, axis_index_groups=groups, tiled=True
    )


def to_partner(x, shards):
    return lax.ppermute(x, "seq", [(i, i ^ 1) for i in range(shards)])


def in_vmem(x):
    return x if INTERPRET else pltpu.with_memory_space_constraint(x, pltpu.VMEM)


def in_hbm(x):
    return x if INTERPRET else pltpu.with_memory_space_constraint(x, pltpu.HBM)


def vmem_out(shape, dtype):
    return jax.ShapeDtypeStruct(shape, dtype) if INTERPRET else pltpu.VMEM(shape, dtype)


def hbm_out(shape, dtype):
    return jax.ShapeDtypeStruct(shape, dtype) if INTERPRET else pltpu.HBM(shape, dtype)


def whole():
    return pl.BlockSpec(memory_space=pltpu.VMEM)


def limit(mib):
    return pltpu.CompilerParams(vmem_limit_bytes=mib << 20)


def project_kernel(hidden_ref, w_query_ref, w_keyval_ref, packet_ref, acc_q, acc_kv):
    step = pl.program_id(0)

    @pl.when(step == 0)
    def _():
        acc_q[...] = jnp.zeros_like(acc_q)
        acc_kv[...] = jnp.zeros_like(acc_kv)

    hidden = hidden_ref[...]
    acc_q[...] += jnp.dot(hidden, w_query_ref[...], preferred_element_type=jnp.float32)
    acc_kv[...] += lax.dot_general(
        hidden, w_keyval_ref[...], (((1,), (1,)), ((), ())), preferred_element_type=jnp.float32
    )

    @pl.when(step == pl.num_programs(0) - 1)
    def _():
        batch, cols = acc_kv.shape
        rows = batch * cols // HEAD_DIM
        keyval = acc_kv[...]
        keyval = jnp.concatenate(
            [keyval[i * rows : (i + 1) * rows] for i in range(HEAD_DIM // cols)], axis=1
        )
        filler = jnp.zeros((PACK_ROWS - batch - rows, HEAD_DIM), jnp.float32)
        packet = jnp.concatenate([acc_q[...], keyval, filler], axis=0).astype(jnp.bfloat16)
        for copy in range(packet_ref.shape[0]):
            packet_ref[copy] = packet


def project(hidden_in, w_query, w_keyval_t, copies):
    batch, width = hidden_in.shape
    cols = w_keyval_t.shape[0]
    steps = 2
    chunk = width // steps
    return pl.pallas_call(
        project_kernel,
        grid=(steps,),
        in_specs=[
            pl.BlockSpec((batch, chunk), lambda k: (0, k)),
            pl.BlockSpec((chunk, HEAD_DIM), lambda k: (k, 0)),
            pl.BlockSpec((cols, chunk), lambda k: (0, k)),
        ],
        out_specs=whole(),
        out_shape=vmem_out((copies, PACK_ROWS, HEAD_DIM), jnp.bfloat16),
        scratch_shapes=[
            pltpu.VMEM((batch, HEAD_DIM), jnp.float32),
            pltpu.VMEM((batch, cols), jnp.float32),
        ],
        compiler_params=limit(8),
        interpret=INTERPRET,
        name="project",
    )(in_hbm(hidden_in), in_hbm(w_query), in_hbm(w_keyval_t))


def new_token(where_ref, own_ref, partner_ref, score_ref, value_ref):
    core, own_group, own_at = where_ref[0], where_ref[1], where_ref[2]
    batch = value_ref.shape[0]
    blocks = own_ref.shape[0] // NEAR
    group_chips = own_ref.shape[0] // (2 * KV_HEADS)
    halves = []
    for half in range(2):
        pieces = []
        for e in range(group_chips):
            chip = (half * KV_HEADS + own_group) * group_chips + e
            at = chip % NEAR * blocks + chip // NEAR
            own = own_ref[at, batch:, :].astype(jnp.float32)
            partner = partner_ref[at, batch:, :].astype(jnp.float32)
            pieces += [jnp.where(core == 0, own, partner), jnp.where(core == 0, partner, own)]
        cols = HEAD_DIM // len(pieces)
        rows = batch * cols // HEAD_DIM
        parts = []
        for q in range(HEAD_DIM // cols):
            lanes = slice(q * cols, (q + 1) * cols)
            parts.append(jnp.concatenate([piece[:rows, lanes] for piece in pieces], axis=1))
        halves.append(jnp.concatenate(parts, axis=0))
    query = own_ref[own_at, :batch, :].astype(jnp.float32)
    score = jnp.sum(query * halves[0], axis=1, keepdims=True) * (1.0 / math.sqrt(HEAD_DIM))
    row = lax.broadcasted_iota(jnp.int32, (batch, HEAD_DIM), 0)
    lane = lax.broadcasted_iota(jnp.int32, (batch, HEAD_DIM), 1)
    score_ref[...] = jnp.sum(jnp.where(row == lane, score, 0.0), axis=0, keepdims=True)
    value_ref[...] = halves[1]


def attend_kernel(where_ref, cached_ref, own_ref, partner_ref, key_ref, value_ref,
                  mine_ref, theirs_ref, level_ref, level_theirs_ref, score_ref, new_value_ref,
                  q_scr, s_scr, o_scr, level_scr, keys_scr, values_scr, sems):
    blocks = own_ref.shape[0] // NEAR
    batch, ctx_dev, _ = key_ref.shape
    group = CORES * NEAR
    pack = group * batch
    parts = batch // STEP_ROWS
    f32, bf16 = jnp.float32, jnp.bfloat16

    def copy_of(kind, part):
        rows = pl.ds(part * STEP_ROWS, STEP_ROWS)
        source, target = ((key_ref, keys_scr), (value_ref, values_scr))[kind]
        return pltpu.make_async_copy(source.at[rows], target.at[rows], sems.at[kind, part])

    for kind in range(2):
        for part in range(parts):
            copy_of(kind, part).start()

    for g in range(blocks):
        for c, ref in enumerate((own_ref, partner_ref)):
            for i in range(NEAR):
                start = g * pack + c * NEAR + i
                tile = ref[i * blocks + g, :batch, :].astype(f32)
                q_scr[pl.ds(start, batch, stride=group), :] = tile
    for g in range(blocks):
        rows = slice(g * pack, (g + 1) * pack)
        q_scr[rows, :] = q_scr[rows, :].T
    new_token(where_ref, own_ref, partner_ref, score_ref, new_value_ref)

    lane_row = lax.broadcasted_iota(jnp.int32, (HEAD_DIM, pack), 1) // group
    s_scr[...] = jnp.zeros_like(s_scr)

    def score_part(part, carry):
        copy_of(0, part).wait()
        for g in range(blocks):
            columns = slice(g * HEAD_DIM, (g + 1) * HEAD_DIM)
            query = q_scr[g * pack : (g + 1) * pack, :]
            total = s_scr[g]
            for j in range(0, STEP_ROWS, 2):
                b = part * STEP_ROWS + j
                keys = jnp.concatenate(
                    [keys_scr[b, :, columns], keys_scr[b + 1, :, columns]], axis=1
                )
                picked = jnp.concatenate(
                    [
                        jnp.where(lane_row == b, query, 0.0).astype(bf16),
                        jnp.where(lane_row == b + 1, query, 0.0).astype(bf16),
                    ],
                    axis=0,
                )
                total += jnp.dot(keys, picked, preferred_element_type=f32)
            s_scr[g] = total
        return carry

    lax.fori_loop(0, parts, score_part, 0)

    level_scr[...] = jnp.full(level_scr.shape, EMPTY, f32)
    slot = lax.broadcasted_iota(jnp.int32, (ctx_dev, pack), 0)
    used = slot < cached_ref[...]
    for g in range(blocks):
        scores = jnp.where(used, s_scr[g] * (1.0 / math.sqrt(HEAD_DIM)), EMPTY)
        top = jnp.max(scores, axis=0, keepdims=True)
        weights = jnp.where(used, jnp.exp(scores - top), 0.0)
        total = jnp.sum(weights, axis=0, keepdims=True)
        some = total > 0
        safe = jnp.where(some, total, 1.0)
        level_scr[g : g + 1, :] = jnp.where(some, top + jnp.log(safe), EMPTY)
        s_scr[g] = (weights / safe).T

    def value_part(part, carry):
        copy_of(1, part).wait()
        for j in range(STEP_ROWS):
            b = part * STEP_ROWS + j
            start = pl.multiple_of(b * group, group)
            for g in range(blocks):
                weights = s_scr[g, pl.ds(start, group), :].astype(bf16)
                values = values_scr[b, :, g * HEAD_DIM : (g + 1) * HEAD_DIM]
                out = jnp.dot(weights, values, preferred_element_type=f32)
                o_scr[pl.ds(g * pack + start, group), :] = out
        return carry

    lax.fori_loop(0, parts, value_part, 0)

    level_scr[...] = level_scr[...].T
    for c, (ref, level) in enumerate(((mine_ref, level_ref), (theirs_ref, level_theirs_ref))):
        for i in range(NEAR):
            at = c * NEAR + i
            rows = slice(i * batch, (i + 1) * batch)
            level[rows, :] = level_scr[pl.ds(at, batch, stride=group), :]
            for g in range(blocks):
                tile = o_scr[pl.ds(g * pack + at, batch, stride=group), :]
                ref[i * blocks + g] = tile.astype(bf16)


def attend(where, cached, own, partner, keys, values):
    batch, ctx_dev, _ = keys.shape
    chips = own.shape[0]
    blocks = chips // NEAR
    pack = CORES * NEAR * batch
    f32, bf16 = jnp.float32, jnp.bfloat16
    return pl.pallas_call(
        attend_kernel,
        grid_spec=pltpu.PrefetchScalarGridSpec(
            num_scalar_prefetch=1,
            grid=(1,),
            in_specs=[whole()] * 3 + [pl.BlockSpec(memory_space=pl.ANY)] * 2,
            out_specs=[whole()] * 6,
            scratch_shapes=[
                pltpu.VMEM((blocks * pack, HEAD_DIM), f32),
                pltpu.VMEM((blocks, ctx_dev, pack), f32),
                pltpu.VMEM((blocks * pack, HEAD_DIM), f32),
                pltpu.VMEM((pack, HEAD_DIM), f32),
                pltpu.VMEM(keys.shape, keys.dtype),
                pltpu.VMEM(values.shape, values.dtype),
                pltpu.SemaphoreType.DMA((2, batch // STEP_ROWS)),
            ],
        ),
        out_shape=[
            vmem_out((chips, batch, HEAD_DIM), bf16),
            vmem_out((chips, batch, HEAD_DIM), bf16),
            vmem_out((NEAR * batch, HEAD_DIM), f32),
            vmem_out((NEAR * batch, HEAD_DIM), f32),
            vmem_out((1, HEAD_DIM), f32),
            vmem_out((batch, HEAD_DIM), f32),
        ],
        compiler_params=limit(24),
        interpret=INTERPRET,
        name="attend",
    )(where, in_vmem(cached), in_vmem(own), in_vmem(partner), in_hbm(keys), in_hbm(values))


def as_columns(*parts):
    count = sum(part.shape[0] for part in parts)
    filler = jnp.zeros((HEAD_DIM - count, HEAD_DIM), jnp.float32)
    return jnp.concatenate([*parts, filler], axis=0).T


def write_packet(ref, at, out, level):
    row = lax.broadcasted_iota(jnp.int32, (PACK_ROWS - out.shape[0], HEAD_DIM), 0)
    high = level.astype(jnp.bfloat16).astype(jnp.float32)
    middle = (level - high).astype(jnp.bfloat16).astype(jnp.float32)
    low = level - high - middle
    stats = jnp.where(row == 0, high, jnp.where(row == 1, middle, jnp.where(row == 2, low, 0.0)))
    ref[at] = jnp.concatenate([out, stats], axis=0).astype(jnp.bfloat16)


def read_levels(ref, batch, scr):
    for r in range(ref.shape[0]):
        stats = ref[r, batch:, :].astype(jnp.float32)
        scr[r : r + 1, :] = stats[0:1] + (stats[1:2] + stats[2:3])
    return scr[...]


def merge_cores_kernel(mine_ref, level_ref, got_ref, got_level_ref, out_ref):
    count, batch, _ = mine_ref.shape
    blocks = count // NEAR
    level, got = level_ref[...], got_level_ref[...]
    top = jnp.maximum(level, got)
    part_a, part_b = jnp.exp(level - top), jnp.exp(got - top)
    total = part_a + part_b
    part_a, part_b = part_a / total, part_b / total
    merged = as_columns(top + jnp.log(total))[:blocks]
    for i in range(NEAR):
        rows = slice(i * batch, (i + 1) * batch)
        levels = pltpu.roll(merged, (HEAD_DIM - i * batch) % HEAD_DIM, 1) if i else merged
        for k in range(blocks):
            r = i * blocks + k
            out = mine_ref[r].astype(jnp.float32) * part_a[rows, k : k + 1]
            out += got_ref[r].astype(jnp.float32) * part_b[rows, k : k + 1]
            write_packet(out_ref, r, out, levels[k : k + 1, :])


def merge_cores(mine, level, got, got_level):
    chips, batch, _ = mine.shape
    return pl.pallas_call(
        merge_cores_kernel,
        in_specs=[whole()] * 4,
        out_specs=whole(),
        out_shape=vmem_out((chips, PACK_ROWS, HEAD_DIM), jnp.bfloat16),
        compiler_params=limit(8),
        interpret=INTERPRET,
        name="merge_cores",
    )(in_vmem(mine), in_vmem(level), in_vmem(got), in_vmem(got_level))


def merge_near_kernel(batch, packet_ref, out_ref, level_scr):
    blocks = out_ref.shape[0]
    levels = read_levels(packet_ref, batch, level_scr)
    parts = [levels[i * blocks : (i + 1) * blocks] for i in range(NEAR)]
    top = functools.reduce(jnp.maximum, parts)
    parts = [jnp.exp(part - top) for part in parts]
    total = functools.reduce(jnp.add, parts)
    merged = top + jnp.log(total)
    columns = as_columns(*[part / total for part in parts])
    for k in range(blocks):
        out = 0.0
        for i in range(NEAR):
            r = i * blocks + k
            rows = packet_ref[r, :batch, :].astype(jnp.float32)
            out += rows * columns[:batch, r : r + 1]
        write_packet(out_ref, k, out, merged[k : k + 1, :])


def merge_near(packets, batch):
    count = packets.shape[0]
    return pl.pallas_call(
        functools.partial(merge_near_kernel, batch),
        in_specs=[whole()],
        out_specs=whole(),
        out_shape=vmem_out((count // NEAR, PACK_ROWS, HEAD_DIM), jnp.bfloat16),
        scratch_shapes=[pltpu.VMEM((count, HEAD_DIM), jnp.float32)],
        compiler_params=limit(8),
        interpret=INTERPRET,
        name="merge_near",
    )(in_vmem(packets))


def merge_far_kernel(packet_ref, score_ref, value_ref, out_ref, level_scr):
    batch = out_ref.shape[0]
    count = packet_ref.shape[0]
    levels = read_levels(packet_ref, batch, level_scr)
    score = score_ref[...]
    top = jnp.maximum(jnp.max(levels, axis=0, keepdims=True), score)
    parts, part_new = jnp.exp(levels - top), jnp.exp(score - top)
    total = jnp.sum(parts, axis=0, keepdims=True) + part_new
    columns = as_columns(parts / total, part_new / total)
    out = value_ref[...] * columns[:batch, count : count + 1]
    for r in range(count):
        out += packet_ref[r, :batch, :].astype(jnp.float32) * columns[:batch, r : r + 1]
    out_ref[...] = out.astype(out_ref.dtype)


def merge_far(packets, score_new, value_new):
    count = packets.shape[0]
    batch = value_new.shape[0]
    return pl.pallas_call(
        merge_far_kernel,
        in_specs=[whole()] * 3,
        out_specs=whole(),
        out_shape=vmem_out((batch, HEAD_DIM), jnp.bfloat16),
        scratch_shapes=[pltpu.VMEM((count, HEAD_DIM), jnp.float32)],
        compiler_params=limit(8),
        interpret=INTERPRET,
        name="merge_far",
    )(in_vmem(packets), in_vmem(score_new), in_vmem(value_new))


def output_kernel(where_ref, attended_ref, w_ref, mine_ref, theirs_ref):
    swap = where_ref[0] == 1
    attended = attended_ref[...]
    for i in range(NEAR):
        start = CORES * i * HEAD_DIM
        term = jnp.dot(
            attended,
            w_ref[:, start : start + CORES * HEAD_DIM],
            preferred_element_type=jnp.float32,
        )
        first, second = term[:, :HEAD_DIM], term[:, HEAD_DIM:]
        mine_ref[i, 0] = jnp.where(swap, second, first).astype(mine_ref.dtype)
        theirs_ref[i, 0] = jnp.where(swap, first, second).astype(theirs_ref.dtype)


def output_terms(where, attended, w_out):
    batch = attended.shape[0]
    rows, width = w_out.shape
    chunk = NEAR * CORES * HEAD_DIM
    blocks = width // chunk
    half = pl.BlockSpec((NEAR, 1, batch, HEAD_DIM), lambda s, *_: (0, s, 0, 0))
    return pl.pallas_call(
        output_kernel,
        grid_spec=pltpu.PrefetchScalarGridSpec(
            num_scalar_prefetch=1,
            grid=(blocks,),
            in_specs=[whole(), pl.BlockSpec((rows, chunk), lambda s, *_: (0, s))],
            out_specs=[half, half],
        ),
        out_shape=[vmem_out((NEAR, blocks, batch, HEAD_DIM), jnp.bfloat16)] * 2,
        compiler_params=limit(8),
        interpret=INTERPRET,
        name="output_terms",
    )(where, in_vmem(attended), w_out)


def body(hidden_in, w_query, w_keyval, key_cache, value_cache, lengths, w_out):
    batch, ctx_dev, half_width = key_cache.shape
    shards = lax.axis_size("seq")
    index = lax.axis_index("seq")
    core = index % CORES
    chips = shards // CORES
    blocks = chips // NEAR
    heads = w_out.shape[0] // HEAD_DIM * shards
    group = heads // KV_HEADS
    f32, bf16 = jnp.float32, jnp.bfloat16

    chip = index // CORES
    own_at = chip % NEAR * blocks + chip // NEAR
    where = jnp.stack([core, index // group, own_at]).astype(jnp.int32)
    cached = jnp.repeat(lengths - index * ctx_dev, group)[None]
    hidden_in, where, cached = lax.optimization_barrier((hidden_in, where, cached))

    packet = project(hidden_in, w_query, w_keyval.T, blocks)
    far = exchange(packet, far_groups(shards))
    near = exchange(
        jnp.broadcast_to(far[None], (NEAR, *far.shape)).reshape(chips, *far.shape[1:]),
        near_groups(shards),
    )
    partner = to_partner(near, shards)

    mine, theirs, level, level_theirs, score_new, value_new = attend(
        where, cached, near, partner, key_cache, value_cache
    )

    got = to_partner(theirs, shards)
    got_level = to_partner(level_theirs, shards)
    packets = exchange(merge_cores(mine, level, got, got_level), near_groups(shards))
    packets = exchange(merge_near(packets, batch), far_groups(shards))
    attended = merge_far(packets, score_new, value_new)

    mine, theirs = output_terms(where, attended, w_out)
    term = (mine.astype(f32) + to_partner(theirs, shards).astype(f32)).astype(bf16)
    arrived = exchange(term.reshape(chips, batch, -1), near_groups(shards))
    term = jnp.sum(arrived.reshape(NEAR, blocks, batch, -1).astype(f32), axis=0).astype(bf16)
    arrived = exchange(term, far_groups(shards))
    return jnp.sum(arrived.astype(f32), axis=0).astype(bf16)


def solution(mesh):
    placed = (
        P("replica", None),
        P(None, "seq"),
        P(None, "seq"),
        P("replica", "seq", None),
        P("replica", "seq", None),
        P("replica"),
        P("seq", None),
    )
    step = jax.shard_map(
        body, mesh=mesh, in_specs=placed, out_specs=P("replica", "seq"), check_vma=False
    )
    return step
```

time: 156 us -> 154 us (0.987)
  blocking collectives: 44.8 us -> 137 us
  waiting for transfers between devices: 45.6 us -> 3.65 us
  starting transfers between devices: 41.2 us -> 0.78 us
  Pallas kernels: 21.9 us -> 10.6 us
    all_to_all x3 -> x6, blocking collectives: 44.8 us -> 137 us  [exchange(): lax.all_to_all(x, 'seq', split_axis=0, concat_axis=0, axis_index_groups=g...]
    all_to_all x3 -> x0, waiting for transfers between devices: 42.2 us -> none  [exchange(): lax.all_to_all(x, 'seq', split_axis=0, concat_axis=0, axis_index_groups=g...]
    all_to_all x3 -> x0, starting transfers between devices: 40.1 us -> none  [exchange(): lax.all_to_all(x, 'seq', split_axis=0, concat_axis=0, axis_index_groups=g...]
    pallas_call x4 -> x1, Pallas kernels: 12 us -> 2.02 us  [output_terms(): pl.pallas_call(output_kernel, grid_spec=pltpu.PrefetchScalarGridSpec(num_...]
    ppermute x5 -> x4, waiting for transfers between devices: 3.43 us -> 3.65 us  [to_partner(): return lax.ppermute(x, 'seq', [(i, i ^ 1) for i in range(shards)])]
  transfers between devices with their start and end apart: 8 -> 4, of which waited for: 6 -> 3; matrix products, arithmetic and copies ran while one was open for 0% -> 0% of each run, Pallas kernels for 8% -> 0%
where the time goes in v5:
time: 154 us; the launch traced here: 153 us
  blocking collectives  137 us (89%)
  Pallas kernels  10.6 us (7%)
  waiting for transfers between devices  3.65 us (2%)
    all_to_all x6, blocking collectives, exchange(): lax.all_to_all(x, 'seq', split_axis=0, concat_axis=0, axis_index_groups=g...  137 us
    pallas_call x1, Pallas kernels, attend(): pl.pallas_call(attend_kernel, grid_spec=pltpu.PrefetchScalarGridSpec(num_...  5.66 us
    ppermute x4, waiting for transfers between devices, to_partner(): return lax.ppermute(x, 'seq', [(i, i ^ 1) for i in range(shards)])  3.65 us
  transfers between devices with their start and end apart: 4, of which 3 were waited for; matrix products, arithmetic and copies ran while one was open for 0% of the time, Pallas kernels for 0%

profile of v5, /device:TPU:38, one launch (start us, length us, event | category | flops | bytes accessed | tf_op | source)
XLA Modules:
  0.0 153.3 jit_solution(12133662606470009745)
XLA Ops:
  0.0 0.7 broadcast_subtract_fusion
  0.7 0.1 broadcast_in_dim.4
  0.7 0.1 broadcast_in_dim_reshape.3.cached_ref
  0.8 0.1 pad_add_fusion.where_ref
  0.9 2.1 %project.1 = bf16[8,24,128]{2,1,0:T(8,128)(2,1)S(1)} custom-call(bf16[16,8192]{1,0:T(8,128)(2,1)} %hidden_ref, bf16[8192,128]{1,0:T(8,128)(2,1)} %w_query_ref.1, bf16[32,8192]{1,0:T(8,128)(2,1)} %bitcast.10), custom_call_target="tpu_custom_call" | custom-call | tf_op jit(solution)/shard_map/project/pallas_call | solution.py:103
  3.1 55.4 %all_to_all.30 = bf16[8,24,128]{2,1,0:T(8,128)(2,1)S(1)} all-to-all(bf16[8,24,128]{2,1,0:T(8,128)(2,1)S(1)} %project.1), channel_id=1, replica_groups={{0,8,16,24,32,40,48,56},{1,9,17,25,33,41,49,57},{2,10,18,26,34,42,50,58..., dimensions={0} | all-to-all | bytes 98304 | tf_op jit(solution)/shard_map/all_to_all | solution.py:37
  58.5 10.5 %all_to_all.31.own_ref = bf16[32,24,128]{2,1,0:T(8,128)(2,1)S(1)} all-to-all(bf16[32,24,128]{2,1,0:T(8,128)(2,1)S(1)} %bitcast.7), channel_id=1, replica_groups={{0,2,4,6},{1,3,5,7},{8,10,12,14},{9,11,13,15},{16,18,20,22},{17,19,21,2..., dimensions={0} | all-to-all | bytes 393216 | tf_op jit(solution)/shard_map/all_to_all | solution.py:37
  69.0 0.0 copy-start
  69.0 0.0 collective-permute-start
  69.0 1.4 collective-permute-done.partner_ref
  70.5 5.7 %attend.1 = (bf16[32,16,128]{2,1,0:T(8,128)(2,1)S(1)}, bf16[32,16,128]{2,1,0:T(8,128)(2,1)S(1)}, f32[64,128]{1,0:T(8,128)S(1)}, f32[64,128]{1,0:T(8,128)S(1)}, f...) custom-call(s32[3]{0:T(128)S(1)} %pad_add_fusion.where_ref, s32[1,128]{1,0:T(1,128)S(1)} %broadcast_in_dim_reshape.3.cached_ref, ...), custom_call_target="tpu_custom_call" | custom-call | tf_op jit(solution)/shard_map/attend/pallas_call | solution.py:253
  76.1 0.3 collective-permute-start.1
  76.4 0.4 collective-permute-start.2
  76.8 0.9 collective-permute-done.2.got_level_ref
  77.7 0.0 collective-permute-done.1.got_ref
  77.7 0.3 merge_cores.1
  78.0 10.6 %all_to_all.32.packet_ref = bf16[32,24,128]{2,1,0:T(8,128)(2,1)S(1)} all-to-all(bf16[32,24,128]{2,1,0:T(8,128)(2,1)S(1)} %merge_cores.1), channel_id=1, replica_groups={{0,2,4,6},{1,3,5,7},{8,10,12,14},{9,11,13,15},{16,18,20,22},{17,19,21,2..., dimensions={0} | all-to-all | bytes 393216 | tf_op jit(solution)/shard_map/all_to_all | solution.py:37
  88.6 0.3 merge_near.1
  88.9 25.3 %all_to_all.33.packet_ref = bf16[8,24,128]{2,1,0:T(8,128)(2,1)S(1)} all-to-all(bf16[8,24,128]{2,1,0:T(8,128)(2,1)S(1)} %merge_near.1), channel_id=1, replica_groups={{0,8,16,24,32,40,48,56},{1,9,17,25,33,41,49,57},{2,10,18,26,34,42,50,58..., dimensions={0} | all-to-all | bytes 98304 | tf_op jit(solution)/shard_map/all_to_all | solution.py:37
  114.2 0.2 merge_far.1.attended_ref
  114.4 0.0 copy-done
  114.4 2.0 %output_terms.1 = (bf16[4,8,16,128]{3,2,1,0:T(8,128)(2,1)S(1)}, bf16[4,8,16,128]{3,2,1,0:T(8,128)(2,1)S(1)}) custom-call(s32[3]{0:T(128)S(1)} %pad_add_fusion.where_ref, bf16[16,128]{1,0:T(8,128)(2,1)S(1)} %merge_far.1.attended_ref, bf16[128,8192]{1,0:T(8,128)(2,1)S(1)} %copy-done), custom_call_target="tpu_custom_call" | custom-call | tf_op jit(solution)/shard_map/output_terms/pallas_call | solution.py:421
  116.5 0.1 collective-permute-start.3
  116.6 1.3 collective-permute-done.3
  118.0 9.6 %all_to_all.34 = bf16[32,16,128]{2,1,0:T(8,128)(2,1)S(1)} all-to-all(bf16[32,16,128]{2,1,0:T(8,128)(2,1)S(1)} %bitcast.8), channel_id=1, replica_groups={{0,2,4,6},{1,3,5,7},{8,10,12,14},{9,11,13,15},{16,18,20,22},{17,19,21,2..., dimensions={0} | all-to-all | bytes 262144 | tf_op jit(solution)/shard_map/all_to_all | solution.py:37
  127.6 25.1 %all_to_all.35 = bf16[8,16,128]{2,1,0:T(8,128)(2,1)S(1)} all-to-all(bf16[8,16,128]{2,1,0:T(8,128)(2,1)S(1)} %reduce_sum.24), channel_id=1, replica_groups={{0,8,16,24,32,40,48,56},{1,9,17,25,33,41,49,57},{2,10,18,26,34,42,50,58..., dimensions={0} | all-to-all | bytes 65536 | tf_op jit(solution)/shard_map/all_to_all | solution.py:37
  152.7 0.6 reduce_sum.25
  (3 shorter events, 0.1 us)
Async XLA Ops:
  69.0 45.4 %copy-start = (bf16[128,8192]{1,0:T(8,128)(2,1)S(1)}, bf16[128,8192]{1,0:T(8,128)(2,1)}, u32[]{:S(2)}) copy-start(bf16[128,8192]{1,0:T(8,128)(2,1)} %w_ref.1) | copy-start | bytes 6291460
  69.0 1.4 collective-permute-start
  76.1 1.5 collective-permute-start.1
  76.4 1.3 collective-permute-start.2
  116.5 1.5 collective-permute-start.3

commit v6 on v5

--- a/solution.py
+++ b/solution.py
@@ -14,6 +14,7 @@
 CORES = 2
 NEAR = 4
 EMPTY = -1e30
+FIRST_EIGHTH = 6
 PACK_ROWS = 24
 STEP_ROWS = 4
 INTERPRET = False
@@ -26,10 +27,18 @@
     ]
 
 
+def block_order(blocks):
+    return [(p + blocks * FIRST_EIGHTH // 8) % blocks for p in range(blocks)]
+
+
+def place_of(block, blocks):
+    return (block + blocks - blocks * FIRST_EIGHTH // 8) % blocks
+
+
 def far_groups(shards):
-    blocks = shards // CORES // NEAR
+    order = block_order(shards // CORES // NEAR)
     return [
-        [CORES * (NEAR * b + i) + c for b in range(blocks)] for i in range(NEAR) for c in range(CORES)
+        [CORES * (NEAR * b + i) + c for b in order] for i in range(NEAR) for c in range(CORES)
     ]
 
 
@@ -130,7 +139,7 @@
         pieces = []
         for e in range(group_chips):
             chip = (half * KV_HEADS + own_group) * group_chips + e
-            at = chip % NEAR * blocks + chip // NEAR
+            at = chip % NEAR * blocks + place_of(chip // NEAR, blocks)
             own = own_ref[at, batch:, :].astype(jnp.float32)
             partner = partner_ref[at, batch:, :].astype(jnp.float32)
             pieces += [jnp.where(core == 0, own, partner), jnp.where(core == 0, partner, own)]
@@ -149,7 +158,7 @@
     value_ref[...] = halves[1]
 
 
-def attend_kernel(where_ref, cached_ref, own_ref, partner_ref, key_ref, value_ref,
+def attend_kernel(where_ref, lengths_ref, own_ref, partner_ref, key_ref, value_ref,
                   mine_ref, theirs_ref, level_ref, level_theirs_ref, score_ref, new_value_ref,
                   q_scr, s_scr, o_scr, level_scr, keys_scr, values_scr, sems):
     blocks = own_ref.shape[0] // NEAR
@@ -157,6 +166,7 @@
     group = CORES * NEAR
     pack = group * batch
     parts = batch // STEP_ROWS
+    order = block_order(blocks)
     f32, bf16 = jnp.float32, jnp.bfloat16
 
     def copy_of(kind, part):
@@ -185,7 +195,7 @@
     def score_part(part, carry):
         copy_of(0, part).wait()
         for g in range(blocks):
-            columns = slice(g * HEAD_DIM, (g + 1) * HEAD_DIM)
+            columns = slice(order[g] * HEAD_DIM, (order[g] + 1) * HEAD_DIM)
             query = q_scr[g * pack : (g + 1) * pack, :]
             total = s_scr[g]
             for j in range(0, STEP_ROWS, 2):
@@ -208,7 +218,10 @@
 
     level_scr[...] = jnp.full(level_scr.shape, EMPTY, f32)
     slot = lax.broadcasted_iota(jnp.int32, (ctx_dev, pack), 0)
-    used = slot < cached_ref[...]
+    cached = jnp.zeros((1, pack), jnp.int32)
+    for b in range(batch):
+        cached = jnp.where(lane_row[:1] == b, lengths_ref[b] - where_ref[3], cached)
+    used = slot < cached
     for g in range(blocks):
         scores = jnp.where(used, s_scr[g] * (1.0 / math.sqrt(HEAD_DIM)), EMPTY)
         top = jnp.max(scores, axis=0, keepdims=True)
@@ -226,7 +239,8 @@
             start = pl.multiple_of(b * group, group)
             for g in range(blocks):
                 weights = s_scr[g, pl.ds(start, group), :].astype(bf16)
-                values = values_scr[b, :, g * HEAD_DIM : (g + 1) * HEAD_DIM]
+                columns = slice(order[g] * HEAD_DIM, (order[g] + 1) * HEAD_DIM)
+                values = values_scr[b, :, columns]
                 out = jnp.dot(weights, values, preferred_element_type=f32)
                 o_scr[pl.ds(g * pack + start, group), :] = out
         return carry
@@ -244,7 +258,7 @@
                 ref[i * blocks + g] = tile.astype(bf16)
 
 
-def attend(where, cached, own, partner, keys, values):
+def attend(where, lengths, own, partner, keys, values):
     batch, ctx_dev, _ = keys.shape
     chips = own.shape[0]
     blocks = chips // NEAR
@@ -253,9 +267,9 @@
     return pl.pallas_call(
         attend_kernel,
         grid_spec=pltpu.PrefetchScalarGridSpec(
-            num_scalar_prefetch=1,
+            num_scalar_prefetch=2,
             grid=(1,),
-            in_specs=[whole()] * 3 + [pl.BlockSpec(memory_space=pl.ANY)] * 2,
+            in_specs=[whole()] * 2 + [pl.BlockSpec(memory_space=pl.ANY)] * 2,
             out_specs=[whole()] * 6,
             scratch_shapes=[
                 pltpu.VMEM((blocks * pack, HEAD_DIM), f32),
@@ -278,7 +292,7 @@
         compiler_params=limit(24),
         interpret=INTERPRET,
         name="attend",
-    )(where, in_vmem(cached), in_vmem(own), in_vmem(partner), in_hbm(keys), in_hbm(values))
+    )(where, lengths, in_vmem(own), in_vmem(partner), in_hbm(keys), in_hbm(values))
 
 
 def as_columns(*parts):
@@ -417,13 +431,17 @@
     rows, width = w_out.shape
     chunk = NEAR * CORES * HEAD_DIM
     blocks = width // chunk
+    turn = block_order(blocks)[0]
     half = pl.BlockSpec((NEAR, 1, batch, HEAD_DIM), lambda s, *_: (0, s, 0, 0))
     return pl.pallas_call(
         output_kernel,
         grid_spec=pltpu.PrefetchScalarGridSpec(
             num_scalar_prefetch=1,
             grid=(blocks,),
-            in_specs=[whole(), pl.BlockSpec((rows, chunk), lambda s, *_: (0, s))],
+            in_specs=[
+                whole(),
+                pl.BlockSpec((rows, chunk), lambda s, *_: (0, (s + turn) % blocks)),
+            ],
             out_specs=[half, half],
         ),
         out_shape=[vmem_out((NEAR, blocks, batch, HEAD_DIM), jnp.bfloat16)] * 2,
@@ -445,10 +463,8 @@
     f32, bf16 = jnp.float32, jnp.bfloat16
 
     chip = index // CORES
-    own_at = chip % NEAR * blocks + chip // NEAR
-    where = jnp.stack([core, index // group, own_at]).astype(jnp.int32)
-    cached = jnp.repeat(lengths - index * ctx_dev, group)[None]
-    hidden_in, where, cached = lax.optimization_barrier((hidden_in, where, cached))
+    own_at = chip % NEAR * blocks + place_of(chip // NEAR, blocks)
+    where = jnp.stack([core, index // group, own_at, index * ctx_dev]).astype(jnp.int32)
 
     packet = project(hidden_in, w_query, w_keyval.T, blocks)
     far = exchange(packet, far_groups(shards))
@@ -459,7 +475,7 @@
     partner = to_partner(near, shards)
 
     mine, theirs, level, level_theirs, score_new, value_new = attend(
-        where, cached, near, partner, key_cache, value_cache
+        where, lengths, near, partner, key_cache, value_cache
     )
 
     got = to_partner(theirs, shards)

time: 154 us -> 144 us (0.935)
  blocking collectives: 137 us -> 128 us
    all_to_all x6, blocking collectives: 137 us -> 128 us  [exchange(): lax.all_to_all(x, 'seq', split_axis=0, concat_axis=0, axis_index_groups=g...]
where the time goes in v6:
time: 144 us
  blocking collectives  128 us (89%)
  Pallas kernels  10.7 us (7%)
  waiting for transfers between devices  3.57 us (2%)
    all_to_all x6, blocking collectives, exchange(): lax.all_to_all(x, 'seq', split_axis=0, concat_axis=0, axis_index_groups=g...  128 us
    pallas_call x1, Pallas kernels, attend(): pl.pallas_call(attend_kernel, grid_spec=pltpu.PrefetchScalarGridSpec(num_...  5.66 us
    ppermute x4, waiting for transfers between devices, to_partner(): return lax.ppermute(x, 'seq', [(i, i ^ 1) for i in range(shards)])  3.57 us
  transfers between devices with their start and end apart: 4, of which 3 were waited for; matrix products, arithmetic and copies ran while one was open for 0% of the time, Pallas kernels for 0%

profile of v6, /device:TPU:38, one launch (start us, length us, event | category | flops | bytes accessed | tf_op | source)
XLA Modules:
  0.0 144.0 jit_solution(17865011240440124739)
XLA Ops:
  0.0 2.1 %project.1 = bf16[8,24,128]{2,1,0:T(8,128)(2,1)S(1)} custom-call(bf16[16,8192]{1,0:T(8,128)(2,1)} %hidden_ref.1, bf16[8192,128]{1,0:T(8,128)(2,1)} %w_query_ref.1, bf16[32,8192]{1,0:T(8,128)(2,1)} %bitcast.11), custom_call_target="tpu_custom_call" | custom-call | tf_op jit(solution)/shard_map/project/pallas_call | solution.py:112
  2.1 45.5 %all_to_all.30 = bf16[8,24,128]{2,1,0:T(8,128)(2,1)S(1)} all-to-all(bf16[8,24,128]{2,1,0:T(8,128)(2,1)S(1)} %project.1), channel_id=1, replica_groups={{48,56,0,8,16,24,32,40},{49,57,1,9,17,25,33,41},{50,58,2,10,18,26,34,42..., dimensions={0} | all-to-all | bytes 98304 | tf_op jit(solution)/shard_map/all_to_all | solution.py:46
  47.7 9.9 %all_to_all.31.own_ref = bf16[32,24,128]{2,1,0:T(8,128)(2,1)S(1)} all-to-all(bf16[32,24,128]{2,1,0:T(8,128)(2,1)S(1)} %bitcast.8), channel_id=1, replica_groups={{0,2,4,6},{1,3,5,7},{8,10,12,14},{9,11,13,15},{16,18,20,22},{17,19,21,2..., dimensions={0} | all-to-all | bytes 393216 | tf_op jit(solution)/shard_map/all_to_all | solution.py:46
  57.5 0.0 collective-permute-start
  57.5 0.1 pad_add_fusion.where_ref
  57.6 0.0 copy-start
  57.6 1.4 collective-permute-done.partner_ref
  59.0 0.0 copy-start.1
  59.0 0.7 copy-done.1
  59.6 5.7 %attend.1 = (bf16[32,16,128]{2,1,0:T(8,128)(2,1)S(1)}, bf16[32,16,128]{2,1,0:T(8,128)(2,1)S(1)}, f32[64,128]{1,0:T(8,128)S(1)}, f32[64,128]{1,0:T(8,128)S(1)}, f...) custom-call(s32[4]{0:T(128)S(1)} %pad_add_fusion.where_ref, s32[16]{0:T(128)S(1)} %copy-done.1, ...), custom_call_target="tpu_custom_call" | custom-call | tf_op jit(solution)/shard_map/attend/pallas_call | solution.py:267
  65.3 0.3 collective-permute-start.1
  65.6 0.4 collective-permute-start.2
  65.9 0.9 collective-permute-done.2.got_level_ref
  66.8 0.0 collective-permute-done.1.got_ref
  66.8 0.3 merge_cores.1
  67.1 10.6 %all_to_all.32.packet_ref = bf16[32,24,128]{2,1,0:T(8,128)(2,1)S(1)} all-to-all(bf16[32,24,128]{2,1,0:T(8,128)(2,1)S(1)} %merge_cores.1), channel_id=1, replica_groups={{0,2,4,6},{1,3,5,7},{8,10,12,14},{9,11,13,15},{16,18,20,22},{17,19,21,2..., dimensions={0} | all-to-all | bytes 393216 | tf_op jit(solution)/shard_map/all_to_all | solution.py:46
  77.8 0.3 merge_near.1
  78.1 27.1 %all_to_all.33.packet_ref = bf16[8,24,128]{2,1,0:T(8,128)(2,1)S(1)} all-to-all(bf16[8,24,128]{2,1,0:T(8,128)(2,1)S(1)} %merge_near.1), channel_id=1, replica_groups={{48,56,0,8,16,24,32,40},{49,57,1,9,17,25,33,41},{50,58,2,10,18,26,34,42..., dimensions={0} | all-to-all | bytes 98304 | tf_op jit(solution)/shard_map/all_to_all | solution.py:46
  105.2 0.2 merge_far.1.attended_ref
  105.4 0.0 copy-done
  105.4 2.1 %output_terms.1 = (bf16[4,8,16,128]{3,2,1,0:T(8,128)(2,1)S(1)}, bf16[4,8,16,128]{3,2,1,0:T(8,128)(2,1)S(1)}) custom-call(s32[4]{0:T(128)S(1)} %pad_add_fusion.where_ref, bf16[16,128]{1,0:T(8,128)(2,1)S(1)} %merge_far.1.attended_ref, bf16[128,8192]{1,0:T(8,128)(2,1)S(1)} %copy-done), custom_call_target="tpu_custom_call" | custom-call | tf_op jit(solution)/shard_map/output_terms/pallas_call | solution.py:436
  107.5 0.1 collective-permute-start.3
  107.7 1.3 collective-permute-done.3
  109.0 8.8 %all_to_all.34 = bf16[32,16,128]{2,1,0:T(8,128)(2,1)S(1)} all-to-all(bf16[32,16,128]{2,1,0:T(8,128)(2,1)S(1)} %bitcast.9), channel_id=1, replica_groups={{0,2,4,6},{1,3,5,7},{8,10,12,14},{9,11,13,15},{16,18,20,22},{17,19,21,2..., dimensions={0} | all-to-all | bytes 262144 | tf_op jit(solution)/shard_map/all_to_all | solution.py:46
  117.9 25.5 %all_to_all.35 = bf16[8,16,128]{2,1,0:T(8,128)(2,1)S(1)} all-to-all(bf16[8,16,128]{2,1,0:T(8,128)(2,1)S(1)} %reduce_sum.24), channel_id=1, replica_groups={{48,56,0,8,16,24,32,40},{49,57,1,9,17,25,33,41},{50,58,2,10,18,26,34,42..., dimensions={0} | all-to-all | bytes 65536 | tf_op jit(solution)/shard_map/all_to_all | solution.py:46
  143.4 0.6 reduce_sum.25
  (3 shorter events, 0.1 us)
Async XLA Ops:
  57.5 1.4 %collective-permute-start = (bf16[32,24,128]{2,1,0:T(8,128)(2,1)S(1)}, bf16[32,24,128]{2,1,0:T(8,128)(2,1)S(1)}, u32[]{:S(2)}, u32[]{:S(2)}) collective-permute-start(bf16[32,24,128]{2,1,0:T(8,128)(2,1)S(1)} %all_to_all.31.own_ref), channel_id=1, source_target_pairs={{0,1},{1,0},{2,3},{3,2},{4,5},{5,4},{6,7},{7,6},{8,9},{9,8},{10,11... | collective-permute-start | bytes 589832 | tf_op jit(solution)/shard_map/ppermute | solution.py:52
  57.6 47.8 %copy-start = (bf16[128,8192]{1,0:T(8,128)(2,1)S(1)}, bf16[128,8192]{1,0:T(8,128)(2,1)}, u32[]{:S(2)}) copy-start(bf16[128,8192]{1,0:T(8,128)(2,1)} %w_ref.1) | copy-start | bytes 6291460
  59.0 0.7 copy-start.1
  65.3 1.5 %collective-permute-start.1 = (bf16[32,16,128]{2,1,0:T(8,128)(2,1)S(1)}, bf16[32,16,128]{2,1,0:T(8,128)(2,1)S(1)}, u32[]{:S(2)}, u32[]{:S(2)}) collective-permute-start(bf16[32,16,128]{2,1,0:T(8,128)(2,1)S(1)} %get-tuple-element.15), channel_id=1, source_target_pairs={{0,1},{1,0},{2,3},{3,2},{4,5},{5,4},{6,7},{7,6},{8,9},{9,8},{10,11... | collective-permute-start | bytes 393224 | tf_op jit(solution)/shard_map/ppermute | solution.py:52
  65.6 1.3 collective-permute-start.2
  107.5 1.5 %collective-permute-start.3 = (bf16[4,8,16,128]{3,2,1,0:T(8,128)(2,1)S(1)}, bf16[4,8,16,128]{3,2,1,0:T(8,128)(2,1)S(1)}, u32[]{:S(2)}, u32[]{:S(2)}) collective-permute-start(bf16[4,8,16,128]{3,2,1,0:T(8,128)(2,1)S(1)} %get-tuple-element.20), channel_id=1, source_target_pairs={{0,1},{1,0},{2,3},{3,2},{4,5},{5,4},{6,7},{7,6},{8,9},{9,8},{10,11... | collective-permute-start | bytes 393224 | tf_op jit(solution)/shard_map/ppermute | solution.py:52

commit v7 on v6

--- a/solution.py
+++ b/solution.py
@@ -14,7 +14,9 @@
 CORES = 2
 NEAR = 4
 EMPTY = -1e30
-FIRST_EIGHTH = 6
+FIRST_EIGHTH = 5
+FIRST_NEAR = 2
+NEAR_ORDER = [(q + FIRST_NEAR) % NEAR for q in range(NEAR)]
 PACK_ROWS = 24
 STEP_ROWS = 4
 INTERPRET = False
@@ -23,7 +25,9 @@
 def near_groups(shards):
     blocks = shards // CORES // NEAR
     return [
-        [CORES * (NEAR * b + i) + c for i in range(NEAR)] for b in range(blocks) for c in range(CORES)
+        [CORES * (NEAR * b + i) + c for i in NEAR_ORDER]
+        for b in range(blocks)
+        for c in range(CORES)
     ]
 
 
@@ -31,8 +35,9 @@
     return [(p + blocks * FIRST_EIGHTH // 8) % blocks for p in range(blocks)]
 
 
-def place_of(block, blocks):
-    return (block + blocks - blocks * FIRST_EIGHTH // 8) % blocks
+def place_of(chip, blocks):
+    near = (chip % NEAR + NEAR - FIRST_NEAR) % NEAR
+    return near * blocks + (chip // NEAR + blocks - blocks * FIRST_EIGHTH // 8) % blocks
 
 
 def far_groups(shards):
@@ -139,7 +144,7 @@
         pieces = []
         for e in range(group_chips):
             chip = (half * KV_HEADS + own_group) * group_chips + e
-            at = chip % NEAR * blocks + place_of(chip // NEAR, blocks)
+            at = place_of(chip, blocks)
             own = own_ref[at, batch:, :].astype(jnp.float32)
             partner = partner_ref[at, batch:, :].astype(jnp.float32)
             pieces += [jnp.where(core == 0, own, partner), jnp.where(core == 0, partner, own)]
@@ -158,9 +163,10 @@
     value_ref[...] = halves[1]
 
 
-def attend_kernel(where_ref, lengths_ref, own_ref, partner_ref, key_ref, value_ref,
+def attend_kernel(where_ref, own_ref, partner_ref, key_ref, value_ref, lengths_ref,
                   mine_ref, theirs_ref, level_ref, level_theirs_ref, score_ref, new_value_ref,
-                  q_scr, s_scr, o_scr, level_scr, keys_scr, values_scr, sems):
+                  q_scr, s_scr, o_scr, level_scr, keys_scr, values_scr, lengths_scr, sems,
+                  lengths_sem):
     blocks = own_ref.shape[0] // NEAR
     batch, ctx_dev, _ = key_ref.shape
     group = CORES * NEAR
@@ -174,6 +180,8 @@
         source, target = ((key_ref, keys_scr), (value_ref, values_scr))[kind]
         return pltpu.make_async_copy(source.at[rows], target.at[rows], sems.at[kind, part])
 
+    lengths_copy = pltpu.make_async_copy(lengths_ref, lengths_scr, lengths_sem)
+    lengths_copy.start()
     for kind in range(2):
         for part in range(parts):
             copy_of(kind, part).start()
@@ -218,9 +226,10 @@
 
     level_scr[...] = jnp.full(level_scr.shape, EMPTY, f32)
     slot = lax.broadcasted_iota(jnp.int32, (ctx_dev, pack), 0)
+    lengths_copy.wait()
     cached = jnp.zeros((1, pack), jnp.int32)
     for b in range(batch):
-        cached = jnp.where(lane_row[:1] == b, lengths_ref[b] - where_ref[3], cached)
+        cached = jnp.where(lane_row[:1] == b, lengths_scr[b] - where_ref[3], cached)
     used = slot < cached
     for g in range(blocks):
         scores = jnp.where(used, s_scr[g] * (1.0 / math.sqrt(HEAD_DIM)), EMPTY)
@@ -267,9 +276,9 @@
     return pl.pallas_call(
         attend_kernel,
         grid_spec=pltpu.PrefetchScalarGridSpec(
-            num_scalar_prefetch=2,
+            num_scalar_prefetch=1,
             grid=(1,),
-            in_specs=[whole()] * 2 + [pl.BlockSpec(memory_space=pl.ANY)] * 2,
+            in_specs=[whole()] * 2 + [pl.BlockSpec(memory_space=pl.ANY)] * 3,
             out_specs=[whole()] * 6,
             scratch_shapes=[
                 pltpu.VMEM((blocks * pack, HEAD_DIM), f32),
@@ -278,7 +287,9 @@
                 pltpu.VMEM((pack, HEAD_DIM), f32),
                 pltpu.VMEM(keys.shape, keys.dtype),
                 pltpu.VMEM(values.shape, values.dtype),
+                pltpu.SMEM(lengths.shape, lengths.dtype),
                 pltpu.SemaphoreType.DMA((2, batch // STEP_ROWS)),
+                pltpu.SemaphoreType.DMA,
             ],
         ),
         out_shape=[
@@ -292,7 +303,14 @@
         compiler_params=limit(24),
         interpret=INTERPRET,
         name="attend",
-    )(where, lengths, in_vmem(own), in_vmem(partner), in_hbm(keys), in_hbm(values))
+    )(
+        where,
+        in_vmem(own),
+        in_vmem(partner),
+        in_hbm(keys),
+        in_hbm(values),
+        in_hbm(lengths),
+    )
 
 
 def as_columns(*parts):
@@ -411,44 +429,38 @@
     )(in_vmem(packets), in_vmem(score_new), in_vmem(value_new))
 
 
-def output_kernel(where_ref, attended_ref, w_ref, mine_ref, theirs_ref):
+def output_kernel(order, where_ref, attended_ref, w_ref, mine_ref, theirs_ref):
     swap = where_ref[0] == 1
     attended = attended_ref[...]
-    for i in range(NEAR):
-        start = CORES * i * HEAD_DIM
-        term = jnp.dot(
-            attended,
-            w_ref[:, start : start + CORES * HEAD_DIM],
-            preferred_element_type=jnp.float32,
-        )
-        first, second = term[:, :HEAD_DIM], term[:, HEAD_DIM:]
-        mine_ref[i, 0] = jnp.where(swap, second, first).astype(mine_ref.dtype)
-        theirs_ref[i, 0] = jnp.where(swap, first, second).astype(theirs_ref.dtype)
+    for p, block in enumerate(order):
+        for q, i in enumerate(NEAR_ORDER):
+            start = (block * NEAR + i) * CORES * HEAD_DIM
+            term = jnp.dot(
+                attended,
+                w_ref[:, start : start + CORES * HEAD_DIM],
+                preferred_element_type=jnp.float32,
+            )
+            first, second = term[:, :HEAD_DIM], term[:, HEAD_DIM:]
+            mine_ref[q, p] = jnp.where(swap, second, first).astype(mine_ref.dtype)
+            theirs_ref[q, p] = jnp.where(swap, first, second).astype(theirs_ref.dtype)
 
 
 def output_terms(where, attended, w_out):
     batch = attended.shape[0]
-    rows, width = w_out.shape
-    chunk = NEAR * CORES * HEAD_DIM
-    blocks = width // chunk
-    turn = block_order(blocks)[0]
-    half = pl.BlockSpec((NEAR, 1, batch, HEAD_DIM), lambda s, *_: (0, s, 0, 0))
+    blocks = w_out.shape[1] // (NEAR * CORES * HEAD_DIM)
     return pl.pallas_call(
-        output_kernel,
+        functools.partial(output_kernel, block_order(blocks)),
         grid_spec=pltpu.PrefetchScalarGridSpec(
             num_scalar_prefetch=1,
-            grid=(blocks,),
-            in_specs=[
-                whole(),
-                pl.BlockSpec((rows, chunk), lambda s, *_: (0, (s + turn) % blocks)),
-            ],
-            out_specs=[half, half],
+            grid=(1,),
+            in_specs=[whole(), whole()],
+            out_specs=[whole(), whole()],
         ),
         out_shape=[vmem_out((NEAR, blocks, batch, HEAD_DIM), jnp.bfloat16)] * 2,
         compiler_params=limit(8),
         interpret=INTERPRET,
         name="output_terms",
-    )(where, in_vmem(attended), w_out)
+    )(where, in_vmem(attended), in_vmem(w_out))
 
 
 def body(hidden_in, w_query, w_keyval, key_cache, value_cache, lengths, w_out):
@@ -463,7 +475,7 @@
     f32, bf16 = jnp.float32, jnp.bfloat16
 
     chip = index // CORES
-    own_at = chip % NEAR * blocks + place_of(chip // NEAR, blocks)
+    own_at = place_of(chip, blocks)
     where = jnp.stack([core, index // group, own_at, index * ctx_dev]).astype(jnp.int32)
 
     packet = project(hidden_in, w_query, w_keyval.T, blocks)

time: 144 us -> 138 us (0.958)
  blocking collectives: 128 us -> 123 us
    all_to_all x6, blocking collectives: 128 us -> 123 us  [exchange(): lax.all_to_all(x, 'seq', split_axis=0, concat_axis=0, axis_index_groups=g...]
where the time goes in v7:
time: 138 us
  blocking collectives  123 us (89%)
  Pallas kernels  9.52 us (7%)
  waiting for transfers between devices  3.57 us (3%)
    all_to_all x6, blocking collectives, exchange(): lax.all_to_all(x, 'seq', split_axis=0, concat_axis=0, axis_index_groups=g...  123 us
    pallas_call x1, Pallas kernels, attend(): pl.pallas_call(attend_kernel, grid_spec=pltpu.PrefetchScalarGridSpec(num_...  5.65 us
    ppermute x4, waiting for transfers between devices, to_partner(): return lax.ppermute(x, 'seq', [(i, i ^ 1) for i in range(shards)])  3.57 us
  transfers between devices with their start and end apart: 4, of which 3 were waited for; matrix products, arithmetic and copies ran while one was open for 0% of the time, Pallas kernels for 0%

profile of v7, /device:TPU:38, one launch (start us, length us, event | category | flops | bytes accessed | tf_op | source)
XLA Modules:
  0.0 137.7 jit_solution(7405824006581271163)
XLA Ops:
  0.0 2.1 %project.1 = bf16[8,24,128]{2,1,0:T(8,128)(2,1)S(1)} custom-call(bf16[16,8192]{1,0:T(8,128)(2,1)} %hidden_ref.1, bf16[8192,128]{1,0:T(8,128)(2,1)} %w_query_ref.1, bf16[32,8192]{1,0:T(8,128)(2,1)} %bitcast.11), custom_call_target="tpu_custom_call" | custom-call | tf_op jit(solution)/shard_map/project/pallas_call | solution.py:117
  2.1 44.9 %all_to_all.30 = bf16[8,24,128]{2,1,0:T(8,128)(2,1)S(1)} all-to-all(bf16[8,24,128]{2,1,0:T(8,128)(2,1)S(1)} %project.1), channel_id=1, replica_groups={{40,48,56,0,8,16,24,32},{41,49,57,1,9,17,25,33},{42,50,58,2,10,18,26,34..., dimensions={0} | all-to-all | bytes 98304 | tf_op jit(solution)/shard_map/all_to_all | solution.py:51
  47.1 8.4 %all_to_all.31.own_ref = bf16[32,24,128]{2,1,0:T(8,128)(2,1)S(1)} all-to-all(bf16[32,24,128]{2,1,0:T(8,128)(2,1)S(1)} %bitcast.8), channel_id=1, replica_groups={{4,6,0,2},{5,7,1,3},{12,14,8,10},{13,15,9,11},{20,22,16,18},{21,23,17,1..., dimensions={0} | all-to-all | bytes 393216 | tf_op jit(solution)/shard_map/all_to_all | solution.py:51
  55.6 0.0 collective-permute-start
  55.6 0.1 pad_add_fusion.where_ref
  55.6 0.0 copy-start
  55.6 1.4 collective-permute-done.partner_ref
  57.0 5.7 %attend.1 = (bf16[32,16,128]{2,1,0:T(8,128)(2,1)S(1)}, bf16[32,16,128]{2,1,0:T(8,128)(2,1)S(1)}, f32[64,128]{1,0:T(8,128)S(1)}, f32[64,128]{1,0:T(8,128)S(1)}, f...) custom-call(s32[4]{0:T(128)S(1)} %pad_add_fusion.where_ref, bf16[32,24,128]{2,1,0:T(8,128)(2,1)S(1)} %all_to_all.31.own_ref, ...), custom_call_target="tpu_custom_call" | custom-call | tf_op jit(solution)/shard_map/attend/pallas_call | solution.py:276
  62.7 0.3 collective-permute-start.1
  62.9 0.4 collective-permute-start.2
  63.3 0.9 collective-permute-done.2.got_level_ref
  64.2 0.0 collective-permute-done.1.got_ref
  64.2 0.3 merge_cores.1
  64.5 9.7 %all_to_all.32.packet_ref = bf16[32,24,128]{2,1,0:T(8,128)(2,1)S(1)} all-to-all(bf16[32,24,128]{2,1,0:T(8,128)(2,1)S(1)} %merge_cores.1), channel_id=1, replica_groups={{4,6,0,2},{5,7,1,3},{12,14,8,10},{13,15,9,11},{20,22,16,18},{21,23,17,1..., dimensions={0} | all-to-all | bytes 393216 | tf_op jit(solution)/shard_map/all_to_all | solution.py:51
  74.2 0.3 merge_near.1
  74.5 26.9 %all_to_all.33.packet_ref = bf16[8,24,128]{2,1,0:T(8,128)(2,1)S(1)} all-to-all(bf16[8,24,128]{2,1,0:T(8,128)(2,1)S(1)} %merge_near.1), channel_id=1, replica_groups={{40,48,56,0,8,16,24,32},{41,49,57,1,9,17,25,33},{42,50,58,2,10,18,26,34..., dimensions={0} | all-to-all | bytes 98304 | tf_op jit(solution)/shard_map/all_to_all | solution.py:51
  101.4 0.2 merge_far.1.attended_ref
  101.6 0.0 copy-done
  101.6 0.9 output_terms.1
  102.6 0.1 collective-permute-start.3
  102.7 1.3 collective-permute-done.3
  104.1 7.6 %all_to_all.34 = bf16[32,16,128]{2,1,0:T(8,128)(2,1)S(1)} all-to-all(bf16[32,16,128]{2,1,0:T(8,128)(2,1)S(1)} %bitcast.9), channel_id=1, replica_groups={{4,6,0,2},{5,7,1,3},{12,14,8,10},{13,15,9,11},{20,22,16,18},{21,23,17,1..., dimensions={0} | all-to-all | bytes 262144 | tf_op jit(solution)/shard_map/all_to_all | solution.py:51
  111.7 25.5 %all_to_all.35 = bf16[8,16,128]{2,1,0:T(8,128)(2,1)S(1)} all-to-all(bf16[8,16,128]{2,1,0:T(8,128)(2,1)S(1)} %reduce_sum.24), channel_id=1, replica_groups={{40,48,56,0,8,16,24,32},{41,49,57,1,9,17,25,33},{42,50,58,2,10,18,26,34..., dimensions={0} | all-to-all | bytes 65536 | tf_op jit(solution)/shard_map/all_to_all | solution.py:51
  137.1 0.6 reduce_sum.25
  (3 shorter events, 0.1 us)
Async XLA Ops:
  55.6 1.4 %collective-permute-start = (bf16[32,24,128]{2,1,0:T(8,128)(2,1)S(1)}, bf16[32,24,128]{2,1,0:T(8,128)(2,1)S(1)}, u32[]{:S(2)}, u32[]{:S(2)}) collective-permute-start(bf16[32,24,128]{2,1,0:T(8,128)(2,1)S(1)} %all_to_all.31.own_ref), channel_id=1, source_target_pairs={{0,1},{1,0},{2,3},{3,2},{4,5},{5,4},{6,7},{7,6},{8,9},{9,8},{10,11... | collective-permute-start | bytes 589832 | tf_op jit(solution)/shard_map/ppermute | solution.py:57
  55.6 46.0 %copy-start = (bf16[128,8192]{1,0:T(8,128)(2,1)S(1)}, bf16[128,8192]{1,0:T(8,128)(2,1)}, u32[]{:S(2)}) copy-start(bf16[128,8192]{1,0:T(8,128)(2,1)} %w_ref.1) | copy-start | bytes 6291460
  62.7 1.5 %collective-permute-start.1 = (bf16[32,16,128]{2,1,0:T(8,128)(2,1)S(1)}, bf16[32,16,128]{2,1,0:T(8,128)(2,1)S(1)}, u32[]{:S(2)}, u32[]{:S(2)}) collective-permute-start(bf16[32,16,128]{2,1,0:T(8,128)(2,1)S(1)} %get-tuple-element.15), channel_id=1, source_target_pairs={{0,1},{1,0},{2,3},{3,2},{4,5},{5,4},{6,7},{7,6},{8,9},{9,8},{10,11... | collective-permute-start | bytes 393224 | tf_op jit(solution)/shard_map/ppermute | solution.py:57
  62.9 1.3 collective-permute-start.2
  102.6 1.5 %collective-permute-start.3 = (bf16[4,8,16,128]{3,2,1,0:T(8,128)(2,1)S(1)}, bf16[4,8,16,128]{3,2,1,0:T(8,128)(2,1)S(1)}, u32[]{:S(2)}, u32[]{:S(2)}) collective-permute-start(bf16[4,8,16,128]{3,2,1,0:T(8,128)(2,1)S(1)} %get-tuple-element.20), channel_id=1, source_target_pairs={{0,1},{1,0},{2,3},{3,2},{4,5},{5,4},{6,7},{7,6},{8,9},{9,8},{10,11... | collective-permute-start | bytes 393224 | tf_op jit(solution)/shard_map/ppermute | solution.py:57

commit v8 on v7

--- a/solution.py
+++ b/solution.py
@@ -14,7 +14,7 @@
 CORES = 2
 NEAR = 4
 EMPTY = -1e30
-FIRST_EIGHTH = 5
+FIRST_EIGHTH = 4
 FIRST_NEAR = 2
 NEAR_ORDER = [(q + FIRST_NEAR) % NEAR for q in range(NEAR)]
 PACK_ROWS = 24

time: 138 us -> 138 us (level)
  no operation moved by 1% of the time
where the time goes in v8:
time: 138 us
  blocking collectives  123 us (89%)
  Pallas kernels  9.55 us (7%)
  waiting for transfers between devices  3.57 us (3%)
    all_to_all x6, blocking collectives, exchange(): lax.all_to_all(x, 'seq', split_axis=0, concat_axis=0, axis_index_groups=g...  123 us
    pallas_call x1, Pallas kernels, attend(): pl.pallas_call(attend_kernel, grid_spec=pltpu.PrefetchScalarGridSpec(num_...  5.68 us
    ppermute x4, waiting for transfers between devices, to_partner(): return lax.ppermute(x, 'seq', [(i, i ^ 1) for i in range(shards)])  3.57 us
  transfers between devices with their start and end apart: 4, of which 3 were waited for; matrix products, arithmetic and copies ran while one was open for 0% of the time, Pallas kernels for 0%

profile of v8, /device:TPU:38, one launch (start us, length us, event | category | flops | bytes accessed | tf_op | source)
XLA Modules:
  0.0 137.8 jit_solution(5262238025378088386)
XLA Ops:
  0.0 2.1 %project.1 = bf16[8,24,128]{2,1,0:T(8,128)(2,1)S(1)} custom-call(bf16[16,8192]{1,0:T(8,128)(2,1)} %hidden_ref.1, bf16[8192,128]{1,0:T(8,128)(2,1)} %w_query_ref.1, bf16[32,8192]{1,0:T(8,128)(2,1)} %bitcast.11), custom_call_target="tpu_custom_call" | custom-call | tf_op jit(solution)/shard_map/project/pallas_call | solution.py:117
  2.1 44.1 %all_to_all.30 = bf16[8,24,128]{2,1,0:T(8,128)(2,1)S(1)} all-to-all(bf16[8,24,128]{2,1,0:T(8,128)(2,1)S(1)} %project.1), channel_id=1, replica_groups={{32,40,48,56,0,8,16,24},{33,41,49,57,1,9,17,25},{34,42,50,58,2,10,18,26..., dimensions={0} | all-to-all | bytes 98304 | tf_op jit(solution)/shard_map/all_to_all | solution.py:51
  46.2 9.6 %all_to_all.31.own_ref = bf16[32,24,128]{2,1,0:T(8,128)(2,1)S(1)} all-to-all(bf16[32,24,128]{2,1,0:T(8,128)(2,1)S(1)} %bitcast.8), channel_id=1, replica_groups={{4,6,0,2},{5,7,1,3},{12,14,8,10},{13,15,9,11},{20,22,16,18},{21,23,17,1..., dimensions={0} | all-to-all | bytes 393216 | tf_op jit(solution)/shard_map/all_to_all | solution.py:51
  55.8 0.0 collective-permute-start
  55.8 0.1 pad_add_fusion.where_ref
  55.9 0.0 copy-start
  55.9 1.4 collective-permute-done.partner_ref
  57.2 5.7 %attend.1 = (bf16[32,16,128]{2,1,0:T(8,128)(2,1)S(1)}, bf16[32,16,128]{2,1,0:T(8,128)(2,1)S(1)}, f32[64,128]{1,0:T(8,128)S(1)}, f32[64,128]{1,0:T(8,128)S(1)}, f...) custom-call(s32[4]{0:T(128)S(1)} %pad_add_fusion.where_ref, bf16[32,24,128]{2,1,0:T(8,128)(2,1)S(1)} %all_to_all.31.own_ref, ...), custom_call_target="tpu_custom_call" | custom-call | tf_op jit(solution)/shard_map/attend/pallas_call | solution.py:276
  62.9 0.3 collective-permute-start.1
  63.2 0.4 collective-permute-start.2
  63.5 0.9 collective-permute-done.2.got_level_ref
  64.4 0.0 collective-permute-done.1.got_ref
  64.4 0.3 merge_cores.1
  64.7 9.7 %all_to_all.32.packet_ref = bf16[32,24,128]{2,1,0:T(8,128)(2,1)S(1)} all-to-all(bf16[32,24,128]{2,1,0:T(8,128)(2,1)S(1)} %merge_cores.1), channel_id=1, replica_groups={{4,6,0,2},{5,7,1,3},{12,14,8,10},{13,15,9,11},{20,22,16,18},{21,23,17,1..., dimensions={0} | all-to-all | bytes 393216 | tf_op jit(solution)/shard_map/all_to_all | solution.py:51
  74.4 0.3 merge_near.1
  74.8 26.6 %all_to_all.33.packet_ref = bf16[8,24,128]{2,1,0:T(8,128)(2,1)S(1)} all-to-all(bf16[8,24,128]{2,1,0:T(8,128)(2,1)S(1)} %merge_near.1), channel_id=1, replica_groups={{32,40,48,56,0,8,16,24},{33,41,49,57,1,9,17,25},{34,42,50,58,2,10,18,26..., dimensions={0} | all-to-all | bytes 98304 | tf_op jit(solution)/shard_map/all_to_all | solution.py:51
  101.3 0.2 merge_far.1.attended_ref
  101.6 0.0 copy-done
  101.6 0.9 output_terms.1
  102.5 0.1 collective-permute-start.3
  102.6 1.3 collective-permute-done.3
  104.0 8.0 %all_to_all.34 = bf16[32,16,128]{2,1,0:T(8,128)(2,1)S(1)} all-to-all(bf16[32,16,128]{2,1,0:T(8,128)(2,1)S(1)} %bitcast.9), channel_id=1, replica_groups={{4,6,0,2},{5,7,1,3},{12,14,8,10},{13,15,9,11},{20,22,16,18},{21,23,17,1..., dimensions={0} | all-to-all | bytes 262144 | tf_op jit(solution)/shard_map/all_to_all | solution.py:51
  112.0 25.1 %all_to_all.35 = bf16[8,16,128]{2,1,0:T(8,128)(2,1)S(1)} all-to-all(bf16[8,16,128]{2,1,0:T(8,128)(2,1)S(1)} %reduce_sum.24), channel_id=1, replica_groups={{32,40,48,56,0,8,16,24},{33,41,49,57,1,9,17,25},{34,42,50,58,2,10,18,26..., dimensions={0} | all-to-all | bytes 65536 | tf_op jit(solution)/shard_map/all_to_all | solution.py:51
  137.2 0.6 reduce_sum.25
  (3 shorter events, 0.1 us)
Async XLA Ops:
  55.8 1.4 %collective-permute-start = (bf16[32,24,128]{2,1,0:T(8,128)(2,1)S(1)}, bf16[32,24,128]{2,1,0:T(8,128)(2,1)S(1)}, u32[]{:S(2)}, u32[]{:S(2)}) collective-permute-start(bf16[32,24,128]{2,1,0:T(8,128)(2,1)S(1)} %all_to_all.31.own_ref), channel_id=1, source_target_pairs={{0,1},{1,0},{2,3},{3,2},{4,5},{5,4},{6,7},{7,6},{8,9},{9,8},{10,11... | collective-permute-start | bytes 589832 | tf_op jit(solution)/shard_map/ppermute | solution.py:57
  55.9 45.7 %copy-start = (bf16[128,8192]{1,0:T(8,128)(2,1)S(1)}, bf16[128,8192]{1,0:T(8,128)(2,1)}, u32[]{:S(2)}) copy-start(bf16[128,8192]{1,0:T(8,128)(2,1)} %w_ref.1) | copy-start | bytes 6291460
  62.9 1.5 %collective-permute-start.1 = (bf16[32,16,128]{2,1,0:T(8,128)(2,1)S(1)}, bf16[32,16,128]{2,1,0:T(8,128)(2,1)S(1)}, u32[]{:S(2)}, u32[]{:S(2)}) collective-permute-start(bf16[32,16,128]{2,1,0:T(8,128)(2,1)S(1)} %get-tuple-element.15), channel_id=1, source_target_pairs={{0,1},{1,0},{2,3},{3,2},{4,5},{5,4},{6,7},{7,6},{8,9},{9,8},{10,11... | collective-permute-start | bytes 393224 | tf_op jit(solution)/shard_map/ppermute | solution.py:57
  63.2 1.3 collective-permute-start.2
  102.5 1.5 %collective-permute-start.3 = (bf16[4,8,16,128]{3,2,1,0:T(8,128)(2,1)S(1)}, bf16[4,8,16,128]{3,2,1,0:T(8,128)(2,1)S(1)}, u32[]{:S(2)}, u32[]{:S(2)}) collective-permute-start(bf16[4,8,16,128]{3,2,1,0:T(8,128)(2,1)S(1)} %get-tuple-element.20), channel_id=1, source_target_pairs={{0,1},{1,0},{2,3},{3,2},{4,5},{5,4},{6,7},{7,6},{8,9},{9,8},{10,11... | collective-permute-start | bytes 393224 | tf_op jit(solution)/shard_map/ppermute | solution.py:57
